TPU v7x, 32 devices: a 4x4x1 block of a 4x4x8 slice. The times are simulated.
32 devices in a mesh: dp: 1 (over z), tp: 4 (over y), cp: 8 (over x, core).
Axes of the slice: x: 4, y: 4, z: 1, core: 2. Of those that a mesh axis runs over, the one named last changes fastest.
The devices are a block of a 4x4x8 slice.
Arguments:
- hidden: bfloat16 [2048, 6144], P(('dp', 'cp'))
- seg_ids: int32 [2048], P(('dp', 'cp'))
- w_q: bfloat16 [6144, 6144], P(None, 'tp')
- b_q: bfloat16 [6144], P('tp')
- w_kv: bfloat16 [6144, 256], replicated
- b_kv: bfloat16 [256], replicated
- w_o: bfloat16 [6144, 6144], P('tp')
- b_o: bfloat16 [6144], replicated
- ln_gain: bfloat16 [6144], replicated
- ln_bias: bfloat16 [6144], replicated
Outputs:
- output 1: bfloat16 [2048, 6144], P(('dp', 'cp'))
- output 2: bfloat16 [2048, 128], P(('dp', 'cp'))
- output 3: bfloat16 [2048, 128], P(('dp', 'cp'))
All inputs are finite; a program needn't handle non-finite values.
Results may differ from a plain program's by a relative error of at most 0.0128034.
Values are sent between devices in bfloat16 or wider.
A program may use at most 768 MiB of HBM per device.

v0:
```python
import jax
import jax.numpy as jnp
from jax import lax
from jax.sharding import PartitionSpec as P, NamedSharding

HEAD_DIM = 128
LN_EPS = 1e-5
ATTN_SCALE = HEAD_DIM ** -0.5


def layer_norm(x_blk, ln_gain, ln_bias):
    x_float = x_blk.astype(jnp.float32)
    centered = x_float - jnp.mean(x_float, axis=-1, keepdims=True)
    variance = jnp.mean(centered * centered, axis=-1, keepdims=True)
    return (centered * lax.rsqrt(variance + LN_EPS) * ln_gain.astype(jnp.float32) + ln_bias.astype(jnp.float32)).astype(jnp.bfloat16)


def merge_block(q_blk, k_blk, v_float, visible, m_prev, l_prev, acc_prev):
    scores = jnp.einsum('bhd,kd->bhk', q_blk, k_blk, preferred_element_type=jnp.float32) * ATTN_SCALE
    scores = jnp.where(visible[:, None, :], scores, -jnp.inf)
    m_new = jnp.maximum(m_prev, jnp.max(scores, axis=-1))
    p_weights = jnp.exp(scores - m_new[..., None])
    rescale = jnp.exp(m_prev - m_new)
    l_new = l_prev * rescale + jnp.sum(p_weights, axis=-1)
    acc_new = acc_prev * rescale[..., None] + jnp.einsum('bhk,kd->bhd', p_weights, v_float, preferred_element_type=jnp.float32)
    return m_new, l_new, acc_new


def solution(mesh):
    n_cp = mesh.shape['cp']
    send_pairs = [(i, i + 1) for i in range(n_cp - 1)]

    def local_block(hidden, seg_ids, w_q, b_q, w_kv, b_kv, w_o, b_o, ln_gain, ln_bias):
        tok_local = hidden.shape[0]
        heads_loc = w_q.shape[1] // HEAD_DIM
        q_rows = min(tok_local, 128)
        n_qblk = tok_local // q_rows
        normed = layer_norm(hidden, ln_gain, ln_bias)
        q_all = (jnp.dot(normed, w_q, preferred_element_type=jnp.float32) + b_q.astype(jnp.float32)).astype(jnp.bfloat16)
        kv_own = (jnp.dot(normed, w_kv, preferred_element_type=jnp.float32) + b_kv.astype(jnp.float32)).astype(jnp.bfloat16)
        q_blocks = q_all.reshape(n_qblk, q_rows, heads_loc, HEAD_DIM)
        seg_blocks = seg_ids.reshape(n_qblk, q_rows)
        pos_local = jnp.arange(tok_local, dtype=jnp.int32)
        pos_blocks = pos_local.reshape(n_qblk, q_rows)
        my_index = lax.axis_index('cp')

        def sweep_keys(kv_blk, seg_keys, causal, is_valid, soft_state):
            k_blk = kv_blk[:, :HEAD_DIM]
            v_float = kv_blk[:, HEAD_DIM:].astype(jnp.float32)

            def one_block(block_in):
                q_blk, seg_q, pos_q, m_prev, l_prev, acc_prev = block_in
                visible = (seg_keys[None, :] == seg_q[:, None]) & is_valid
                if causal:
                    visible = visible & (pos_local[None, :] <= pos_q[:, None])
                return merge_block(q_blk, k_blk, v_float, visible, m_prev, l_prev, acc_prev)

            return tuple(lax.map(one_block, (q_blocks, seg_blocks, pos_blocks) + tuple(soft_state)))

        m_init = jnp.full((n_qblk, q_rows, heads_loc), -1e30, jnp.float32)
        l_init = jnp.zeros((n_qblk, q_rows, heads_loc), jnp.float32)
        acc_init = jnp.zeros((n_qblk, q_rows, heads_loc, HEAD_DIM), jnp.float32)
        own_state = sweep_keys(kv_own, seg_ids, True, True, (m_init, l_init, acc_init))

        def shift_step(step_idx, loop_carry):
            kv_blk, seg_keys, m_prev, l_prev, acc_prev = loop_carry
            kv_blk = lax.ppermute(kv_blk, 'cp', send_pairs)
            seg_keys = lax.ppermute(seg_keys, 'cp', send_pairs)
            new_state = sweep_keys(kv_blk, seg_keys, False, my_index >= step_idx, (m_prev, l_prev, acc_prev))
            return (kv_blk, seg_keys) + new_state

        loop_out = lax.fori_loop(1, n_cp, shift_step, (kv_own, seg_ids) + own_state)
        attn_out = (loop_out[4] / loop_out[3][..., None]).astype(jnp.bfloat16).reshape(tok_local, heads_loc * HEAD_DIM)
        partial = jnp.dot(attn_out, w_o, preferred_element_type=jnp.float32).astype(jnp.bfloat16)
        proj_sum = lax.psum(partial, 'tp')
        y_out = (hidden.astype(jnp.float32) + proj_sum.astype(jnp.float32) + b_o.astype(jnp.float32)).astype(jnp.bfloat16)
        return y_out, kv_own[:, :HEAD_DIM], kv_own[:, HEAD_DIM:]

    row_spec = P(('dp', 'cp'), None)
    tok_spec = P(('dp', 'cp'))
    mapped = jax.shard_map(local_block, mesh=mesh,
                           in_specs=(row_spec, tok_spec, P(None, 'tp'), P('tp'), P(None, None), P(None), P('tp', None), P(None), P(None), P(None)),
                           out_specs=(row_spec, row_spec, row_spec), check_vma=False)
    return mapped
```

profile of v0, /device:TPU:102, one launch (start us, length us, event | category | flops | bytes accessed | tf_op | source)
XLA Modules:
  0.0 258.0 jit_solution(13990647872911928374)
XLA Ops:
  9.8 2.4 convert_reduce_fusion
  13.3 10.0 %fusion.42 = bf16[256,1536]{1,0:T(8,128)(2,1)} fusion(bf16[6144,1536]{1,0:T(8,128)(2,1)} %param.18, f32[1536]{0:T(1024)S(1)} %convert_element_type.56, bf16[256,6144]{1,0:T(8,128)(2,1)S(1)} %copy-done.5, f32[6144]{0:T(1024)S(1)} %convert_element_type.52, f32[6144]{0:T(1024)S(1)} %convert_element_type.51, f32[256]{0:T(256)S(1)} %add_rsqrt_fusion, ...), kind=kOutput, calls=%fused_computation.67 | convolution fusion | flops 4842061824 | bytes 22863872 | tf_op jit(solution)/shard_map/dot_general | solution.py:39
  28.0 3.2 %fusion.43 = bf16[256,256]{1,0:T(8,128)(2,1)S(1)} fusion(bf16[6144,256]{1,0:T(8,128)(2,1)S(1)} %copy-done, f32[256]{0:T(256)S(1)} %convert_element_type.54, bf16[256,6144]{1,0:T(8,128)(2,1)} %param.16, f32[6144]{0:T(1024)S(1)} %convert_element_type.52, f32[6144]{0:T(1024)S(1)} %convert_element_type.51, f32[256]{0:T(256)S(1)} %add_rsqrt_fusion, ...), kind=kOutput, calls=%fused_computation.70 | convolution fusion | flops 814874624 | bytes 6474752 | tf_op jit(solution)/shard_map/dot_general | solution.py:40
  31.9 8.7 %while.67 = (s32[]{:T(128)}, f32[2,128,12]{1,2,0:T(8,128)S(1)}, f32[2,128,12]{1,2,0:T(8,128)S(1)}, f32[2,128,12,128]{3,1,2,0:T(8,128)}, s32[256]{0:T(256)S(1)}, ...) while((s32[]{:T(128)}, f32[2,128,12]{1,2,0:T(8,128)S(1)}, ...), condition=%wide.region_5.6_spmd.clone, body=%wide.region_2.5_spmd.clone.sunk | while | flops 203988480 | bytes 18768060 | solution.py:58
  41.2 114.6 %while.66 = (s32[]{:T(128)}, bf16[256,256]{1,0:T(8,128)(2,1)}, s32[256]{0:T(256)S(1)}, f32[2,128,12]{1,2,0:T(8,128)S(1)}, f32[2,128,12]{1,2,0:T(8,128)S(1)}, /*i...) while((s32[]{:T(128)}, bf16[256,256]{1,0:T(8,128)(2,1)}, ...), condition=%wide.region_11.12_spmd, body=%wide.region_6.11_spmd.sunk | while | flops 204150784 | bytes 22203376 | solution.py:72
  45.1 3.0 %collective-permute-done.1 = s32[256]{0:T(256)S(1)} collective-permute-done((s32[256]{0:T(256)S(1)}, s32[256]{0:T(256)S(1)}, u32[]{:S(2)}, u32[]{:S(2)}) %collective-permute-start.1) | collective-permute-done | bytes 1056 | tf_op jit(solution)/shard_map/while/body/eval_jaxpr/ppermute | solution.py:68
  48.1 8.8 %while.68 = (s32[]{:T(128)}, f32[2,128,12]{1,2,0:T(8,128)S(1)}, f32[2,128,12]{1,2,0:T(8,128)S(1)}, f32[2,128,12,128]{3,1,2,0:T(8,128)}, s32[256]{0:T(256)S(1)}, ...) while((s32[]{:T(128)}, f32[2,128,12]{1,2,0:T(8,128)S(1)}, ...), condition=%wide.region_10.10_spmd.clone, body=%wide.region_7.9_spmd.clone.sunk | while | flops 204150784 | bytes 21148356 | solution.py:58
  61.5 3.0 %collective-permute-done.1 = s32[256]{0:T(256)S(1)} collective-permute-done((s32[256]{0:T(256)S(1)}, s32[256]{0:T(256)S(1)}, u32[]{:S(2)}, u32[]{:S(2)}) %collective-permute-start.1) | collective-permute-done | bytes 1056 | tf_op jit(solution)/shard_map/while/body/eval_jaxpr/ppermute | solution.py:68
  64.5 8.8 %while.68 = (s32[]{:T(128)}, f32[2,128,12]{1,2,0:T(8,128)S(1)}, f32[2,128,12]{1,2,0:T(8,128)S(1)}, f32[2,128,12,128]{3,1,2,0:T(8,128)}, s32[256]{0:T(256)S(1)}, ...) while((s32[]{:T(128)}, f32[2,128,12]{1,2,0:T(8,128)S(1)}, ...), condition=%wide.region_10.10_spmd.clone, body=%wide.region_7.9_spmd.clone.sunk | while | flops 204150784 | bytes 21148356 | solution.py:58
  77.9 3.0 %collective-permute-done.1 = s32[256]{0:T(256)S(1)} collective-permute-done((s32[256]{0:T(256)S(1)}, s32[256]{0:T(256)S(1)}, u32[]{:S(2)}, u32[]{:S(2)}) %collective-permute-start.1) | collective-permute-done | bytes 1056 | tf_op jit(solution)/shard_map/while/body/eval_jaxpr/ppermute | solution.py:68
  80.9 8.8 %while.68 = (s32[]{:T(128)}, f32[2,128,12]{1,2,0:T(8,128)S(1)}, f32[2,128,12]{1,2,0:T(8,128)S(1)}, f32[2,128,12,128]{3,1,2,0:T(8,128)}, s32[256]{0:T(256)S(1)}, ...) while((s32[]{:T(128)}, f32[2,128,12]{1,2,0:T(8,128)S(1)}, ...), condition=%wide.region_10.10_spmd.clone, body=%wide.region_7.9_spmd.clone.sunk | while | flops 204150784 | bytes 21148356 | solution.py:58
  94.2 3.0 %collective-permute-done.1 = s32[256]{0:T(256)S(1)} collective-permute-done((s32[256]{0:T(256)S(1)}, s32[256]{0:T(256)S(1)}, u32[]{:S(2)}, u32[]{:S(2)}) %collective-permute-start.1) | collective-permute-done | bytes 1056 | tf_op jit(solution)/shard_map/while/body/eval_jaxpr/ppermute | solution.py:68
  97.2 8.8 %while.68 = (s32[]{:T(128)}, f32[2,128,12]{1,2,0:T(8,128)S(1)}, f32[2,128,12]{1,2,0:T(8,128)S(1)}, f32[2,128,12,128]{3,1,2,0:T(8,128)}, s32[256]{0:T(256)S(1)}, ...) while((s32[]{:T(128)}, f32[2,128,12]{1,2,0:T(8,128)S(1)}, ...), condition=%wide.region_10.10_spmd.clone, body=%wide.region_7.9_spmd.clone.sunk | while | flops 204150784 | bytes 21148356 | solution.py:58
  110.6 3.0 %collective-permute-done.1 = s32[256]{0:T(256)S(1)} collective-permute-done((s32[256]{0:T(256)S(1)}, s32[256]{0:T(256)S(1)}, u32[]{:S(2)}, u32[]{:S(2)}) %collective-permute-start.1) | collective-permute-done | bytes 1056 | tf_op jit(solution)/shard_map/while/body/eval_jaxpr/ppermute | solution.py:68
  113.6 8.8 %while.68 = (s32[]{:T(128)}, f32[2,128,12]{1,2,0:T(8,128)S(1)}, f32[2,128,12]{1,2,0:T(8,128)S(1)}, f32[2,128,12,128]{3,1,2,0:T(8,128)}, s32[256]{0:T(256)S(1)}, ...) while((s32[]{:T(128)}, f32[2,128,12]{1,2,0:T(8,128)S(1)}, ...), condition=%wide.region_10.10_spmd.clone, body=%wide.region_7.9_spmd.clone.sunk | while | flops 204150784 | bytes 21148356 | solution.py:58
  127.0 3.0 %collective-permute-done.1 = s32[256]{0:T(256)S(1)} collective-permute-done((s32[256]{0:T(256)S(1)}, s32[256]{0:T(256)S(1)}, u32[]{:S(2)}, u32[]{:S(2)}) %collective-permute-start.1) | collective-permute-done | bytes 1056 | tf_op jit(solution)/shard_map/while/body/eval_jaxpr/ppermute | solution.py:68
  130.0 8.8 %while.68 = (s32[]{:T(128)}, f32[2,128,12]{1,2,0:T(8,128)S(1)}, f32[2,128,12]{1,2,0:T(8,128)S(1)}, f32[2,128,12,128]{3,1,2,0:T(8,128)}, s32[256]{0:T(256)S(1)}, ...) while((s32[]{:T(128)}, f32[2,128,12]{1,2,0:T(8,128)S(1)}, ...), condition=%wide.region_10.10_spmd.clone, body=%wide.region_7.9_spmd.clone.sunk | while | flops 204150784 | bytes 21148356 | solution.py:58
  143.3 3.0 %collective-permute-done.1 = s32[256]{0:T(256)S(1)} collective-permute-done((s32[256]{0:T(256)S(1)}, s32[256]{0:T(256)S(1)}, u32[]{:S(2)}, u32[]{:S(2)}) %collective-permute-start.1) | collective-permute-done | bytes 1056 | tf_op jit(solution)/shard_map/while/body/eval_jaxpr/ppermute | solution.py:68
  146.3 8.8 %while.68 = (s32[]{:T(128)}, f32[2,128,12]{1,2,0:T(8,128)S(1)}, f32[2,128,12]{1,2,0:T(8,128)S(1)}, f32[2,128,12,128]{3,1,2,0:T(8,128)}, s32[256]{0:T(256)S(1)}, ...) while((s32[]{:T(128)}, f32[2,128,12]{1,2,0:T(8,128)S(1)}, ...), condition=%wide.region_10.10_spmd.clone, body=%wide.region_7.9_spmd.clone.sunk | while | flops 204150784 | bytes 21148356 | solution.py:58
  155.8 2.8 %divide_convert_fusion = bf16[2,128,12,128]{3,1,2,0:T(8,128)(2,1)} fusion(f32[2,128,12,128]{3,1,2,0:T(8,128)} %get-tuple-element.295, f32[2,128,12]{1,2,0:T(8,128)S(1)} %get-tuple-element.296), kind=kLoop, calls=%fused_computation.68 | loop fusion | flops 786432 | bytes 2371584 | tf_op jit(solution)/shard_map/convert_element_type | solution.py:73
  158.6 3.0 %copy.18 = bf16[2,128,12,128]{1,0,3,2:T(2,128)(2,1)} copy(bf16[2,128,12,128]{3,1,2,0:T(8,128)(2,1)} %divide_convert_fusion) | data formatting | bytes 1572864 | tf_op jit(solution)/shard_map/convert_element_type | solution.py:73
  161.6 10.4 %convolution_convert_fusion = bf16[256,6144]{1,0:T(8,128)(2,1)} fusion(bf16[1536,6144]{1,0:T(8,128)(2,1)} %param.22, bf16[192,8,2,128]{3,2,1,0:T(2,128)(2,1)} %bitcast.116), kind=kOutput, calls=%fused_computation.57 | convolution fusion | flops 4833411072 | bytes 22806528 | tf_op jit(solution)/shard_map/dot_general | solution.py:74
  172.7 72.7 %all-reduce.2.cloned.1.call-done = bf16[256,6144]{1,0:T(8,128)(2,1)} async-done(((bf16[256,6144]{1,0:T(8,128)(2,1)}), bf16[256,6144]{1,0:T(8,128)(2,1)}) %all-reduce.2.cloned.1.call-update) | async-done | bytes 3145744 | tf_op jit(solution)/shard_map/psum | solution.py:75
  245.4 5.7 %fusion.41 = bf16[256,6144]{1,0:T(8,128)(2,1)} fusion(bf16[256,6144]{1,0:T(8,128)(2,1)} %param.16, bf16[256,6144]{1,0:T(8,128)(2,1)} %all-reduce.2.cloned.1.call-done, f32[6144]{0:T(1024)S(1)} %convert_element_type.62), kind=kLoop, calls=%fused_computation.65 | loop fusion | flops 7864320 | bytes 9461760 | tf_op jit(solution)/shard_map/convert_element_type | solution.py:76
  (266 shorter events, 111.4 us)
Async XLA Ops:
  7.2 20.9 %copy-start = (bf16[6144,256]{1,0:T(8,128)(2,1)S(1)}, bf16[6144,256]{1,0:T(8,128)(2,1)}, u32[]{:S(2)}) copy-start(bf16[6144,256]{1,0:T(8,128)(2,1)} %param.20) | copy-start | bytes 9437188
  7.2 238.2 %all-reduce.2.cloned.1.call-start = ((), (), s32[]{:S(2)}) async-start(), calls=%async_computation | async-start | bytes 6291456 | tf_op jit(solution)/shard_map/psum | solution.py:75
  7.3 5.0 %copy-start.5 = (bf16[256,6144]{1,0:T(8,128)(2,1)S(1)}, bf16[256,6144]{1,0:T(8,128)(2,1)}, u32[]{:S(2)}) copy-start(bf16[256,6144]{1,0:T(8,128)(2,1)} %param.16) | copy-start | bytes 9437188
  9.8 3.4 %copy-start.9 = (s32[256]{0:T(256)S(1)}, s32[256]{0:T(256)}, u32[]{:S(2)}) copy-start(s32[256]{0:T(256)} %param.17) | copy-start | bytes 3076
  9.8 3.4 %copy-start.11 = (bf16[1536]{0:T(1024)(128)(2,1)S(1)}, bf16[1536]{0:T(1024)(128)(2,1)}, u32[]{:S(2)}) copy-start(bf16[1536]{0:T(1024)(128)(2,1)} %param.19) | copy-start | bytes 9220
  41.2 6.9 %collective-permute-start = (bf16[256,256]{1,0:T(8,128)(2,1)}, bf16[256,256]{1,0:T(8,128)(2,1)S(1)}, u32[]{:S(2)}, u32[]{:S(2)}) collective-permute-start(bf16[256,256]{1,0:T(8,128)(2,1)} %get-tuple-element.772), channel_id=1, source_target_pairs={{0,1},{1,2},{2,3},{3,4},{4,5},{5,6},{6,7},{8,9},{9,10},{10,11},{11... | collective-permute-start | bytes 393224 | tf_op jit(solution)/shard_map/while/body/eval_jaxpr/ppermute | solution.py:67
  43.2 4.9 %collective-permute-start.1 = (s32[256]{0:T(256)S(1)}, s32[256]{0:T(256)S(1)}, u32[]{:S(2)}, u32[]{:S(2)}) collective-permute-start(s32[256]{0:T(256)S(1)} %get-tuple-element.773), channel_id=1, source_target_pairs={{0,1},{1,2},{2,3},{3,4},{4,5},{5,6},{6,7},{8,9},{9,10},{10,11},{11... | collective-permute-start | bytes 3080 | tf_op jit(solution)/shard_map/while/body/eval_jaxpr/ppermute | solution.py:68
  48.1 2.3 copy-start.3
  57.6 6.9 %collective-permute-start = (bf16[256,256]{1,0:T(8,128)(2,1)}, bf16[256,256]{1,0:T(8,128)(2,1)S(1)}, u32[]{:S(2)}, u32[]{:S(2)}) collective-permute-start(bf16[256,256]{1,0:T(8,128)(2,1)} %get-tuple-element.772), channel_id=1, source_target_pairs={{0,1},{1,2},{2,3},{3,4},{4,5},{5,6},{6,7},{8,9},{9,10},{10,11},{11... | collective-permute-start | bytes 393224 | tf_op jit(solution)/shard_map/while/body/eval_jaxpr/ppermute | solution.py:67
  59.5 4.9 %collective-permute-start.1 = (s32[256]{0:T(256)S(1)}, s32[256]{0:T(256)S(1)}, u32[]{:S(2)}, u32[]{:S(2)}) collective-permute-start(s32[256]{0:T(256)S(1)} %get-tuple-element.773), channel_id=1, source_target_pairs={{0,1},{1,2},{2,3},{3,4},{4,5},{5,6},{6,7},{8,9},{9,10},{10,11},{11... | collective-permute-start | bytes 3080 | tf_op jit(solution)/shard_map/while/body/eval_jaxpr/ppermute | solution.py:68
  64.5 2.3 copy-start.3
  74.0 6.9 %collective-permute-start = (bf16[256,256]{1,0:T(8,128)(2,1)}, bf16[256,256]{1,0:T(8,128)(2,1)S(1)}, u32[]{:S(2)}, u32[]{:S(2)}) collective-permute-start(bf16[256,256]{1,0:T(8,128)(2,1)} %get-tuple-element.772), channel_id=1, source_target_pairs={{0,1},{1,2},{2,3},{3,4},{4,5},{5,6},{6,7},{8,9},{9,10},{10,11},{11... | collective-permute-start | bytes 393224 | tf_op jit(solution)/shard_map/while/body/eval_jaxpr/ppermute | solution.py:67
  75.9 4.9 %collective-permute-start.1 = (s32[256]{0:T(256)S(1)}, s32[256]{0:T(256)S(1)}, u32[]{:S(2)}, u32[]{:S(2)}) collective-permute-start(s32[256]{0:T(256)S(1)} %get-tuple-element.773), channel_id=1, source_target_pairs={{0,1},{1,2},{2,3},{3,4},{4,5},{5,6},{6,7},{8,9},{9,10},{10,11},{11... | collective-permute-start | bytes 3080 | tf_op jit(solution)/shard_map/while/body/eval_jaxpr/ppermute | solution.py:68
  80.9 2.3 copy-start.3
  90.3 6.9 %collective-permute-start = (bf16[256,256]{1,0:T(8,128)(2,1)}, bf16[256,256]{1,0:T(8,128)(2,1)S(1)}, u32[]{:S(2)}, u32[]{:S(2)}) collective-permute-start(bf16[256,256]{1,0:T(8,128)(2,1)} %get-tuple-element.772), channel_id=1, source_target_pairs={{0,1},{1,2},{2,3},{3,4},{4,5},{5,6},{6,7},{8,9},{9,10},{10,11},{11... | collective-permute-start | bytes 393224 | tf_op jit(solution)/shard_map/while/body/eval_jaxpr/ppermute | solution.py:67
  92.3 4.9 %collective-permute-start.1 = (s32[256]{0:T(256)S(1)}, s32[256]{0:T(256)S(1)}, u32[]{:S(2)}, u32[]{:S(2)}) collective-permute-start(s32[256]{0:T(256)S(1)} %get-tuple-element.773), channel_id=1, source_target_pairs={{0,1},{1,2},{2,3},{3,4},{4,5},{5,6},{6,7},{8,9},{9,10},{10,11},{11... | collective-permute-start | bytes 3080 | tf_op jit(solution)/shard_map/while/body/eval_jaxpr/ppermute | solution.py:68
  97.2 2.3 copy-start.3
  106.7 6.9 %collective-permute-start = (bf16[256,256]{1,0:T(8,128)(2,1)}, bf16[256,256]{1,0:T(8,128)(2,1)S(1)}, u32[]{:S(2)}, u32[]{:S(2)}) collective-permute-start(bf16[256,256]{1,0:T(8,128)(2,1)} %get-tuple-element.772), channel_id=1, source_target_pairs={{0,1},{1,2},{2,3},{3,4},{4,5},{5,6},{6,7},{8,9},{9,10},{10,11},{11... | collective-permute-start | bytes 393224 | tf_op jit(solution)/shard_map/while/body/eval_jaxpr/ppermute | solution.py:67
  108.6 4.9 %collective-permute-start.1 = (s32[256]{0:T(256)S(1)}, s32[256]{0:T(256)S(1)}, u32[]{:S(2)}, u32[]{:S(2)}) collective-permute-start(s32[256]{0:T(256)S(1)} %get-tuple-element.773), channel_id=1, source_target_pairs={{0,1},{1,2},{2,3},{3,4},{4,5},{5,6},{6,7},{8,9},{9,10},{10,11},{11... | collective-permute-start | bytes 3080 | tf_op jit(solution)/shard_map/while/body/eval_jaxpr/ppermute | solution.py:68
  123.1 6.9 %collective-permute-start = (bf16[256,256]{1,0:T(8,128)(2,1)}, bf16[256,256]{1,0:T(8,128)(2,1)S(1)}, u32[]{:S(2)}, u32[]{:S(2)}) collective-permute-start(bf16[256,256]{1,0:T(8,128)(2,1)} %get-tuple-element.772), channel_id=1, source_target_pairs={{0,1},{1,2},{2,3},{3,4},{4,5},{5,6},{6,7},{8,9},{9,10},{10,11},{11... | collective-permute-start | bytes 393224 | tf_op jit(solution)/shard_map/while/body/eval_jaxpr/ppermute | solution.py:67
  125.0 4.9 %collective-permute-start.1 = (s32[256]{0:T(256)S(1)}, s32[256]{0:T(256)S(1)}, u32[]{:S(2)}, u32[]{:S(2)}) collective-permute-start(s32[256]{0:T(256)S(1)} %get-tuple-element.773), channel_id=1, source_target_pairs={{0,1},{1,2},{2,3},{3,4},{4,5},{5,6},{6,7},{8,9},{9,10},{10,11},{11... | collective-permute-start | bytes 3080 | tf_op jit(solution)/shard_map/while/body/eval_jaxpr/ppermute | solution.py:68
  130.0 2.3 copy-start.3
  139.4 6.9 %collective-permute-start = (bf16[256,256]{1,0:T(8,128)(2,1)}, bf16[256,256]{1,0:T(8,128)(2,1)S(1)}, u32[]{:S(2)}, u32[]{:S(2)}) collective-permute-start(bf16[256,256]{1,0:T(8,128)(2,1)} %get-tuple-element.772), channel_id=1, source_target_pairs={{0,1},{1,2},{2,3},{3,4},{4,5},{5,6},{6,7},{8,9},{9,10},{10,11},{11... | collective-permute-start | bytes 393224 | tf_op jit(solution)/shard_map/while/body/eval_jaxpr/ppermute | solution.py:67
  141.4 4.9 %collective-permute-start.1 = (s32[256]{0:T(256)S(1)}, s32[256]{0:T(256)S(1)}, u32[]{:S(2)}, u32[]{:S(2)}) collective-permute-start(s32[256]{0:T(256)S(1)} %get-tuple-element.773), channel_id=1, source_target_pairs={{0,1},{1,2},{2,3},{3,4},{4,5},{5,6},{6,7},{8,9},{9,10},{10,11},{11... | collective-permute-start | bytes 3080 | tf_op jit(solution)/shard_map/while/body/eval_jaxpr/ppermute | solution.py:68
  (31 other events, 45.7 us)
Sparse Core Ops, SparseCore 0:
  172.2 73.1 all-reduce.1
where the time goes:
time: 260 us; the launch traced here: 258 us
  waiting for transfers between devices  93.5 us (36%)
  matrix products  63.5 us (24%)
  local copies, waits for them, and re-layouts  33.6 us (13%)
  starting transfers between devices  27.3 us (10%)
  other arithmetic  24.6 us (9%)
  between operations  14.2 us (5%)
    psum x1, waiting for transfers between devices, local_block(): proj_sum = lax.psum(partial, 'tp')  72.7 us
    dot_general x16, matrix products, merge_block(): jnp.einsum('bhd,kd->bhk', q_blk, k_blk, preferred_element_type=jnp.float32)  25.1 us
    while x78, local copies, waits for them, and re-layouts  22.8 us
    ppermute x7, waiting for transfers between devices, shift_step(): seg_keys = lax.ppermute(seg_keys, 'cp', send_pairs)  20.7 us
    dot_general x16, matrix products, merge_block(): jnp.einsum('bhk,kd->bhd', p_weights, v_float, preferred_element_type=jnp....  14.7 us
    ppermute x7, starting transfers between devices, shift_step(): seg_keys = lax.ppermute(seg_keys, 'cp', send_pairs)  13.7 us
    ppermute x7, starting transfers between devices, shift_step(): kv_blk = lax.ppermute(kv_blk, 'cp', send_pairs)  13.6 us
    dot_general x1, matrix products, local_block(): jnp.dot(attn_out, w_o, preferred_element_type=jnp.float32)  10.4 us
  transfers between devices with their start and end apart: 15, of which 8 were waited for; matrix products, arithmetic and copies ran while one was open for 0% of the time, Pallas kernels for 0%

commit v1 on v0

v1 whole, which is shorter than its diff:
```python
import functools

import jax
import jax.numpy as jnp
from jax import lax
from jax.experimental import pallas as pl
from jax.experimental.pallas import tpu as pltpu
from jax.sharding import PartitionSpec as P

HEAD_DIM = 128
LN_EPS = 1e-5
SCORE_EXP2 = HEAD_DIM ** -0.5 * 1.4426950408889634
PIECE = 64
SEG_ROWS = 16
MESH_ID = pl.DeviceIdType.MESH
F32 = jnp.float32
BF16 = jnp.bfloat16


def each(lo, hi, body):
    def step(i, carry):
        body(i)
        return carry
    lax.fori_loop(lo, hi, step, 0)


def block_kernel(n_tp, n_cp, hid_hbm, seg_ref, wq_hbm, bq_ref, wkv_hbm, bkv_ref, wo_hbm, bo_ref, gain_ref, lnb_ref,
                 y_hbm, k_ref, v_ref,
                 hid, normed, gain_b, bias_b, wkv, wq, wo, kvbuf, segq, q_s, m_s, l_s, acc_s, o_s, stage, recv, y_v,
                 hid_sem, wkv_sem, wq_sem, wo_sem, kv_send, fwd_send, kv_recv, msg_send, msg_recv,
                 ag_send, ag_recv, fw_send, fw_recv, out_sem):
    tok, d_model = hid.shape
    n_heads = q_s.shape[1] // PIECE
    n_piece = tok // PIECE
    n_chip = n_cp // 2
    chunk = d_model // n_tp
    half = chunk // 2
    me_t = lax.axis_index('tp')
    me_c = lax.axis_index('cp')
    chip = me_c // 2
    core = me_c % 2
    sibling = me_c + 1 - 2 * core
    right = (me_t + 1) % n_tp
    left = (me_t + n_tp - 1) % n_tp
    across = (me_t + 2) % n_tp

    ln_rows = tok // 4
    def load_hid(i):
        rows = pl.ds(i * ln_rows, ln_rows)
        return pltpu.make_async_copy(hid_hbm.at[rows, :], hid.at[rows, :], hid_sem.at[i])
    def load_wkv():
        return pltpu.make_async_copy(wkv_hbm, wkv, wkv_sem)
    def load_wq(i):
        return pltpu.make_async_copy(wq_hbm.at[:, pl.ds(i * 256, 256)], wq.at[i], wq_sem.at[i])
    slots = ((across, 0), (across, 1), (right, 1), (left, 0), (right, 0), (left, 1), (me_t, 0), (me_t, 1))
    def load_wo(i):
        owner, part = slots[i]
        cols = pl.ds(pl.multiple_of(owner * chunk + part * half, 128), half)
        return pltpu.make_async_copy(wo_hbm.at[:, cols], wo.at[i], wo_sem.at[i])
    for i in range(4):
        load_hid(i).start()
    load_wkv().start()
    for i in range(wq.shape[0]):
        load_wq(i).start()
    for i in range(8):
        load_wo(i).start()

    barrier = pltpu.get_barrier_semaphore()
    peers = [{'tp': left}, {'tp': right}, {'cp': sibling}] + [{'cp': (me_c + 2 * d) % n_cp} for d in range(1, n_chip)]
    for peer in peers:
        pl.semaphore_signal(barrier, inc=1, device_id=peer, device_id_type=MESH_ID)

    gain_b[...] = jnp.broadcast_to(gain_ref[...].astype(F32), gain_b.shape)
    bias_b[...] = jnp.broadcast_to(lnb_ref[...].astype(F32), bias_b.shape)
    for i in range(4):
        load_hid(i).wait()
        def norm_rows(r, i=i):
            rows = pl.ds(pl.multiple_of(i * ln_rows + r * 16, 16), 16)
            x = hid[rows, :].astype(F32)
            centered = x - jnp.mean(x, axis=-1, keepdims=True)
            variance = jnp.mean(centered * centered, axis=-1, keepdims=True)
            normed[rows, :] = (centered * lax.rsqrt(variance + LN_EPS) * gain_b[...] + bias_b[...]).astype(BF16)
        each(0, ln_rows // 16, norm_rows)

    seg = seg_ref[...]
    seg_high = (seg // 256).astype(F32)
    seg_low = (seg % 256).astype(F32)
    row_id = lax.broadcasted_iota(jnp.int32, (SEG_ROWS, tok), 0)
    kvbuf[me_c, tok:, :] = jnp.where(row_id == 0, seg_high, jnp.where(row_id == 1, seg_low, 0.0)).astype(BF16)
    seg_f = seg.astype(F32)
    for b in range(tok // 128):
        column = jnp.broadcast_to(seg_f[:, b * 128:(b + 1) * 128], (128, 128)).T
        for s in range(128 // PIECE):
            part = column[s * PIECE:(s + 1) * PIECE]
            segq[b * (128 // PIECE) + s] = jnp.concatenate([part] * (tok // 128), axis=1)

    load_wkv().wait()
    kv = (jnp.dot(normed[...], wkv[...], preferred_element_type=F32) + bkv_ref[...].astype(F32)).astype(BF16)
    kvbuf[me_c, :tok, :] = kv
    k_ref[...] = kv[:, :HEAD_DIM]
    v_ref[...] = kv[:, HEAD_DIM:]
    pl.semaphore_wait(barrier, len(peers))

    def send_kv(block, target, send_sem):
        return pltpu.make_async_remote_copy(src_ref=kvbuf.at[block], dst_ref=kvbuf.at[block], send_sem=send_sem,
                                            recv_sem=kv_recv.at[block], device_id={'cp': target}, device_id_type=MESH_ID)
    for d in range(n_chip - 1, 0, -1):
        @pl.when(chip + d < n_chip)
        def _(d=d):
            send_kv(me_c, (me_c + 2 * d) % n_cp, kv_send.at[d]).start()
    @pl.when(core == 0)
    def _():
        send_kv(me_c, sibling, kv_send.at[0]).start()

    for i in range(wq.shape[0]):
        load_wq(i).wait()
        q = (jnp.dot(normed[...], wq[i], preferred_element_type=F32) + bq_ref[:, i * 256:(i + 1) * 256].astype(F32)).astype(BF16)
        for piece in range(n_piece):
            for h in range(2):
                q_s[piece, (2 * i + h) * PIECE:(2 * i + h + 1) * PIECE, :] = q[piece * PIECE:(piece + 1) * PIECE, h * HEAD_DIM:(h + 1) * HEAD_DIM]

    def attend(piece, block, first):
        q = q_s[piece]
        k_blk = kvbuf[block, :tok, :HEAD_DIM]
        v_blk = kvbuf[block, :tok, HEAD_DIM:]
        digits = kvbuf[block, tok:, :].astype(F32)
        seg_key = digits[0:1] * 256.0 + digits[1:2]
        visible = segq[piece] == seg_key
        if first:
            q_pos = lax.broadcasted_iota(jnp.int32, (PIECE, tok), 0) + piece * PIECE
            visible = visible & (lax.broadcasted_iota(jnp.int32, (PIECE, tok), 1) <= q_pos)
        s = lax.dot_general(q, k_blk, (((1,), (1,)), ((), ())), preferred_element_type=F32)
        s = jnp.where(visible[None], s.reshape(n_heads, PIECE, tok), -jnp.inf).reshape(n_heads * PIECE, tok)
        m_new = jnp.broadcast_to(jnp.max(s, axis=-1, keepdims=True), (n_heads * PIECE, HEAD_DIM))
        if not first:
            m_prev = m_s[piece]
            m_new = jnp.maximum(m_prev, m_new)
        weights = jnp.exp2((s - jnp.concatenate([m_new] * (tok // HEAD_DIM), axis=1)) * SCORE_EXP2)
        total = jnp.broadcast_to(jnp.sum(weights, axis=-1, keepdims=True), (n_heads * PIECE, HEAD_DIM))
        out = jnp.dot(weights.astype(BF16), v_blk, preferred_element_type=F32)
        m_s[piece] = m_new
        if first:
            l_s[piece] = total
            acc_s[piece] = out
        else:
            rescale = jnp.exp2((m_prev - m_new) * SCORE_EXP2)
            l_s[piece] = l_s[piece] * rescale + total
            acc_s[piece] = acc_s[piece] * rescale + out

    each(0, n_piece, lambda piece: attend(piece, me_c, True))
    @pl.when(core == 1)
    def _():
        send_kv(sibling, sibling, kv_send.at[0]).wait_recv()
        each(0, n_piece, lambda piece: attend(piece, sibling, False))

    def take_far(i):
        same = me_c - 2 * (i + 1)
        other = sibling - 2 * (i + 1)
        passing = send_kv(same, sibling, fwd_send.at[i])
        passing.wait_recv()
        passing.start()
        attend(0, same, False)
        send_kv(other, sibling, fwd_send.at[i]).wait_recv()
        attend(0, other, False)
    each(0, chip, take_far)

    def message(piece, i):
        target = (me_t + 1 + (i % 2) * (n_tp - 2)) % n_tp
        return pltpu.make_async_remote_copy(src_ref=stage.at[piece, i], dst_ref=recv.at[piece, i], send_sem=msg_send.at[piece, i],
                                            recv_sem=msg_recv.at[piece, i], device_id={'tp': target}, device_id_type=MESH_ID)
    def y_part(piece, owner, part):
        return y_v.at[pl.ds(pl.multiple_of(piece * PIECE, PIECE), PIECE), pl.ds(pl.multiple_of(owner * chunk + part * half, 128), half)]
    def gather(piece, way, part):
        ref = y_part(piece, me_t, part)
        return pltpu.make_async_remote_copy(src_ref=ref, dst_ref=ref, send_sem=ag_send.at[piece, way, part],
                                            recv_sem=ag_recv.at[piece, way, part], device_id={'tp': (right, left)[way]}, device_id_type=MESH_ID)
    def pass_on(piece, way):
        ref = y_part(piece, (left, right)[way], way)
        return pltpu.make_async_remote_copy(src_ref=ref, dst_ref=ref, send_sem=fw_send.at[piece, way],
                                            recv_sem=fw_recv.at[piece, way], device_id={'tp': (right, left)[way]}, device_id_type=MESH_ID)
    def put_out(piece):
        rows = pl.ds(pl.multiple_of(piece * PIECE, PIECE), PIECE)
        return pltpu.make_async_copy(y_v.at[rows, :], y_hbm.at[rows, :], out_sem.at[piece])

    for i in range(8):
        load_wo(i).wait()

    def step(s):
        @pl.when(s < n_piece)
        def _():
            @pl.when(s > 0)
            def _():
                each(0, 2 * chip, lambda block: attend(s, block, False))
            attn = (acc_s[s] / l_s[s]).astype(BF16)
            for h in range(n_heads):
                o_s[:, h * HEAD_DIM:(h + 1) * HEAD_DIM] = attn[h * PIECE:(h + 1) * PIECE]
            def project(i):
                stage[s, i] = jnp.dot(o_s[...], wo[i], preferred_element_type=F32).astype(BF16)
                @pl.when(i < 4)
                def _():
                    message(s, i).start()
            each(0, 8, project)
            for i in range(2):
                message(s, i).wait_recv()
                stage[s, 4 + i] = (stage[s, 4 + i].astype(F32) + recv[s, i].astype(F32)).astype(BF16)
                message(s, 4 + i).start()

        @pl.when((s >= 1) & (s < n_piece + 1))
        def _():
            piece = s - 1
            for i in range(2, 6):
                message(piece, i).wait_recv()
            rows = pl.ds(pl.multiple_of(piece * PIECE, PIECE), PIECE)
            for part in range(2):
                cols = pl.ds(pl.multiple_of(me_t * chunk + part * half, 128), half)
                from_left, from_right = ((4, 3), (2, 5))[part]
                proj = stage[piece, 6 + part].astype(F32) + recv[piece, from_left].astype(F32) + recv[piece, from_right].astype(F32)
                y_v[rows, cols] = (hid[rows, cols].astype(F32) + proj + bo_ref[:, cols].astype(F32)).astype(BF16)
                for way in range(2):
                    gather(piece, way, part).start()

        @pl.when((s >= 2) & (s < n_piece + 2))
        def _():
            piece = s - 2
            for way in range(2):
                gather(piece, way, way).wait_recv()
                pass_on(piece, way).start()

        @pl.when(s >= 3)
        def _():
            piece = s - 3
            for way in range(2):
                gather(piece, way, 1 - way).wait_recv()
                pass_on(piece, way).wait_recv()
            put_out(piece).start()
    each(0, n_piece + 3, step)

    def finish(piece):
        for i in range(6):
            message(piece, i).wait_send()
        for way in range(2):
            for part in range(2):
                gather(piece, way, part).wait_send()
            pass_on(piece, way).wait_send()
        put_out(piece).wait()
    each(0, n_piece, finish)
    for d in range(n_chip - 1, 0, -1):
        @pl.when(chip + d < n_chip)
        def _(d=d):
            send_kv(me_c, (me_c + 2 * d) % n_cp, kv_send.at[d]).wait_send()
    @pl.when(core == 0)
    def _():
        send_kv(me_c, sibling, kv_send.at[0]).wait_send()
    each(0, chip, lambda i: send_kv(me_c - 2 * (i + 1), sibling, fwd_send.at[i]).wait_send())


def solution(mesh):
    n_tp, n_cp = mesh.shape['tp'], mesh.shape['cp']

    def local_block(hidden, seg_ids, w_q, b_q, w_kv, b_kv, w_o, b_o, ln_gain, ln_bias):
        tok, d_model = hidden.shape
        width = w_q.shape[1]
        n_piece = tok // PIECE
        n_heads = width // HEAD_DIM
        rows = n_heads * PIECE
        half = d_model // n_tp // 2
        hbm = pl.BlockSpec(memory_space=pl.ANY)
        vmem = pl.BlockSpec(memory_space=pltpu.VMEM)
        dma = pltpu.SemaphoreType.DMA
        scratch = [
            pltpu.VMEM((tok, d_model), BF16),
            pltpu.VMEM((tok, d_model), BF16),
            pltpu.VMEM((16, d_model), F32),
            pltpu.VMEM((16, d_model), F32),
            pltpu.VMEM((d_model, 2 * HEAD_DIM), BF16),
            pltpu.VMEM((width // 256, d_model, 256), BF16),
            pltpu.VMEM((2 * n_tp, width, half), BF16),
            pltpu.VMEM((n_cp, tok + SEG_ROWS, 2 * HEAD_DIM), BF16),
            pltpu.VMEM((n_piece, PIECE, tok), F32),
            pltpu.VMEM((n_piece, rows, HEAD_DIM), BF16),
            pltpu.VMEM((n_piece, rows, HEAD_DIM), F32),
            pltpu.VMEM((n_piece, rows, HEAD_DIM), F32),
            pltpu.VMEM((n_piece, rows, HEAD_DIM), F32),
            pltpu.VMEM((PIECE, width), BF16),
            pltpu.VMEM((n_piece, 8, PIECE, half), BF16),
            pltpu.VMEM((n_piece, 6, PIECE, half), BF16),
            pltpu.VMEM((tok, d_model), BF16),
            dma((4,)), dma, dma((width // 256,)), dma((8,)),
            dma((n_cp // 2,)), dma((n_cp // 2,)), dma((n_cp,)), dma((n_piece, 6)), dma((n_piece, 6)),
            dma((n_piece, 2, 2)), dma((n_piece, 2, 2)), dma((n_piece, 2)), dma((n_piece, 2)), dma((n_piece,)),
        ]
        row = lambda a: a.reshape(1, a.shape[0])
        return pl.pallas_call(
            functools.partial(block_kernel, n_tp, n_cp),
            out_shape=(jax.ShapeDtypeStruct((tok, d_model), BF16), jax.ShapeDtypeStruct((tok, HEAD_DIM), BF16),
                       jax.ShapeDtypeStruct((tok, HEAD_DIM), BF16)),
            in_specs=[hbm, vmem, hbm, vmem, hbm, vmem, hbm, vmem, vmem, vmem],
            out_specs=(hbm, vmem, vmem),
            scratch_shapes=scratch,
            compiler_params=pltpu.CompilerParams(collective_id=0, has_side_effects=True, vmem_limit_bytes=67043328),
            name='attention_block',
        )(hidden, row(seg_ids), w_q, row(b_q), w_kv, row(b_kv), w_o, row(b_o), row(ln_gain), row(ln_bias))

    row_spec = P(('dp', 'cp'), None)
    tok_spec = P(('dp', 'cp'))
    return jax.shard_map(local_block, mesh=mesh,
                         in_specs=(row_spec, tok_spec, P(None, 'tp'), P('tp'), P(None, None), P(None), P('tp', None), P(None), P(None), P(None)),
                         out_specs=(row_spec, row_spec, row_spec), check_vma=False)
```

time: 260 us -> 109 us (0.42)
  Pallas kernels: 0 us -> 95.9 us
  waiting for transfers between devices: 93.5 us -> 0 us
  matrix products: 63.5 us -> 0 us
  starting transfers between devices: 27.3 us -> 0 us
  other arithmetic: 24.6 us -> 0 us
  local copies, waits for them, and re-layouts: 33.6 us -> 11.7 us
  between operations: 14.2 us -> 0.66 us
    pallas_call x0 -> x1, Pallas kernels: none -> 95.9 us  [local_block(): pl.pallas_call(functools.partial(block_kernel, n_tp, n_cp), out_shape=(ja...]
    psum x1 -> x0, waiting for transfers between devices: 72.7 us -> none  [local_block(): proj_sum = lax.psum(partial, 'tp')]
    dot_general x35 -> x0, matrix products: 63.5 us -> none  [the longest x16 25.1 us: merge_block(): jnp.einsum('bhd,kd->bhk', q_blk, k_blk, preferred_element_type=jnp.float32)]
    ppermute x14 -> x0, starting transfers between devices: 27.2 us -> none  [the longest x7 13.7 us: shift_step(): seg_keys = lax.ppermute(seg_keys, 'cp', send_pairs)]
    while x78 -> x0, local copies, waits for them, and re-layouts: 22.8 us -> none
    ppermute x14 -> x0, waiting for transfers between devices: 20.7 us -> none  [the longest x7 20.7 us: shift_step(): seg_keys = lax.ppermute(seg_keys, 'cp', send_pairs)]
    reduce_sum x18 -> x0, other arithmetic: 11.6 us -> none  [the longest x16 8.18 us: merge_block(): l_new = l_prev * rescale + jnp.sum(p_weights, axis=-1)]
    convert_element_type x7 -> x0, other arithmetic: 11 us -> none  [the longest x1 5.68 us: local_block(): (hidden.astype(jnp.float32) + proj_sum.astype(jnp.float32) + b_o.astype(j...]
  transfers between devices with their start and end apart: 15 -> 0, of which waited for: 8 -> 0; matrix products, arithmetic and copies ran while one was open for 0% -> 0% of each run, Pallas kernels for 0% -> 0%
where the time goes in v1:
time: 109 us; the launch traced here: 108 us
  Pallas kernels  95.9 us (88%)
  local copies, waits for them, and re-layouts  11.7 us (11%)
    pallas_call x1, Pallas kernels, local_block(): pl.pallas_call(functools.partial(block_kernel, n_tp, n_cp), out_shape=(ja...  95.9 us
    reshape x5, local copies, waits for them, and re-layouts, local_block(): row = lambda a: a.reshape(1, a.shape[0])  6.5 us
    unnamed x7, local copies, waits for them, and re-layouts  5.18 us

profile of v1, /device:TPU:102, one launch (start us, length us, event | category | flops | bytes accessed | tf_op | source)
XLA Modules:
  0.0 108.2 jit_solution(13139618849581468452)
XLA Ops:
  0.6 1.2 %reshape.26.bkv_ref = bf16[1,256]{1,0:T(2,128)(2,1)} reshape(bf16[256]{0:T(256)(128)(2,1)} %param.15) | data formatting | bytes 1024 | tf_op jit(solution)/shard_map/reshape | solution.py:292
  1.9 1.3 %reshape.25.bq_ref = bf16[1,1536]{1,0:T(2,128)(2,1)} reshape(bf16[1536]{0:T(1024)(128)(2,1)} %param.13) | data formatting | bytes 6144 | tf_op jit(solution)/shard_map/reshape | solution.py:292
  3.1 1.3 %reshape.27.bo_ref = bf16[1,6144]{1,0:T(2,128)(2,1)} reshape(bf16[6144]{0:T(1024)(128)(2,1)} %param.17) | data formatting | bytes 24576 | tf_op jit(solution)/shard_map/reshape | solution.py:292
  4.5 1.3 %reshape.28.gain_ref = bf16[1,6144]{1,0:T(2,128)(2,1)} reshape(bf16[6144]{0:T(1024)(128)(2,1)} %param.18) | data formatting | bytes 24576 | tf_op jit(solution)/shard_map/reshape | solution.py:292
  5.8 1.3 %reshape.29.lnb_ref = bf16[1,6144]{1,0:T(2,128)(2,1)} reshape(bf16[6144]{0:T(1024)(128)(2,1)} %param.19) | data formatting | bytes 24576 | tf_op jit(solution)/shard_map/reshape | solution.py:292
  7.1 95.9 %attention_block.1 = (bf16[256,6144]{1,0:T(8,128)(2,1)}, bf16[256,128]{1,0:T(8,128)(2,1)}, bf16[256,128]{1,0:T(8,128)(2,1)}) custom-call(bf16[256,6144]{1,0:T(8,128)(2,1)} %hid_hbm.1, s32[1,256]{1,0:T(1,128)} %bitcast.1, bf16[6144,1536]{1,0:T(8,128)(2,1)} %wq_hbm.1, bf16[1,1536]{1,0:T(2,128)(2,1)} %reshape.25.bq_ref, bf16[6144,256]{1,0:T(8,128)(2,1)} %wkv_hbm.1, ...), custom_call_target="tpu_custom_call" | custom-call | tf_op jit(solution)/shard_map/attention_block/pallas_call | solution.py:293
  103.0 0.0 copy-start.1
  103.1 0.0 copy-start
  103.1 3.9 %copy.16 = bf16[256,6144]{1,0:T(8,128)(2,1)} copy(bf16[256,6144]{1,0:T(8,128)(2,1)} %get-tuple-element.6) | data formatting | bytes 6291456
  107.0 0.0 copy-done.1
  107.0 0.6 copy.17
  107.6 0.0 copy-done
  107.6 0.6 copy.18
Async XLA Ops:
  103.0 3.9 %copy-start.1 = (bf16[256,128]{1,0:T(8,128)(2,1)S(1)}, bf16[256,128]{1,0:T(8,128)(2,1)}, u32[]{:S(2)}) copy-start(bf16[256,128]{1,0:T(8,128)(2,1)} %get-tuple-element.7) | copy-start | bytes 196612
  103.1 4.6 %copy-start = (bf16[256,128]{1,0:T(8,128)(2,1)S(1)}, bf16[256,128]{1,0:T(8,128)(2,1)}, u32[]{:S(2)}) copy-start(bf16[256,128]{1,0:T(8,128)(2,1)} %get-tuple-element.8) | copy-start | bytes 196612

commit v2 on v1

v2 whole, which is shorter than its diff:
```python
import functools

import jax
import jax.numpy as jnp
from jax import lax
from jax.experimental import pallas as pl
from jax.experimental.pallas import tpu as pltpu
from jax.sharding import PartitionSpec as P

HEAD_DIM = 128
LN_EPS = 1e-5
SCORE_EXP2 = HEAD_DIM ** -0.5 * 1.4426950408889634
PIECE = 64
Q_COLS = 512
VMEM_LIMIT = 60 * 2 ** 20
SEG_ROWS = 16
MESH_ID = pl.DeviceIdType.MESH
F32 = jnp.float32
BF16 = jnp.bfloat16


def each(lo, hi, body):
    def step(i, carry):
        body(i)
        return carry
    lax.fori_loop(lo, hi, step, 0)


def block_kernel(n_tp, n_cp, hid_hbm, seg_ref, wq_hbm, bq_ref, wkv_hbm, bkv_ref, wo_hbm, bo_ref, gain_ref, lnb_ref,
                 y_v, k_ref, v_ref,
                 normed, gain_f, bias_f, bq_f, bo_f, wkv, wq, wo, kvbuf, segq, q_s, s_buf, m_s, l_s, acc_s, o_s, stage, recv,
                 hid_sem, wkv_sem, wq_sem, wo_sem, kv_send, fwd_send, kv_recv, msg_send, msg_recv,
                 ag_send, ag_recv, fw_send, fw_recv):
    hid = y_v
    tok, d_model = hid.shape
    n_heads = q_s.shape[1] // PIECE
    n_piece = tok // PIECE
    n_chip = n_cp // 2
    chunk = d_model // n_tp
    half = chunk // 2
    q_cols = wq.shape[2]
    n_q = wq.shape[0]
    me_t = lax.axis_index('tp')
    me_c = lax.axis_index('cp')
    chip = me_c // 2
    core = me_c % 2
    sibling = me_c + 1 - 2 * core
    right = (me_t + 1) % n_tp
    left = (me_t + n_tp - 1) % n_tp
    across = (me_t + 2) % n_tp

    ln_rows = tok // 4
    def load_hid(i):
        rows = pl.ds(i * ln_rows, ln_rows)
        return pltpu.make_async_copy(hid_hbm.at[rows, :], hid.at[rows, :], hid_sem.at[i])
    def load_wkv():
        return pltpu.make_async_copy(wkv_hbm, wkv, wkv_sem)
    def load_wq(i):
        return pltpu.make_async_copy(wq_hbm.at[:, pl.ds(i * q_cols, q_cols)], wq.at[i], wq_sem.at[i])
    slots = ((across, 0), (across, 1), (right, 1), (left, 0), (right, 0), (left, 1), (me_t, 0), (me_t, 1))
    def load_wo(i):
        owner, part = slots[i]
        cols = pl.ds(pl.multiple_of(owner * chunk + part * half, 128), half)
        return pltpu.make_async_copy(wo_hbm.at[:, cols], wo.at[i], wo_sem.at[i])
    def wait_wo(i):
        pltpu.make_async_copy(wo_hbm.at[:, pl.ds(0, half)], wo.at[i], wo_sem.at[i]).wait()
    for i in range(4):
        load_hid(i).start()

    barrier = pltpu.get_barrier_semaphore()
    peers = [{'tp': left}, {'tp': right}, {'cp': sibling}] + [{'cp': (me_c + 2 * d) % n_cp} for d in range(1, n_chip)]
    for peer in peers:
        pl.semaphore_signal(barrier, inc=1, device_id=peer, device_id_type=MESH_ID)

    gain_f[...] = gain_ref[...].astype(F32).reshape(gain_f.shape)
    bias_f[...] = lnb_ref[...].astype(F32).reshape(bias_f.shape)
    for i in range(4):
        with jax.named_scope('hid_wait'):
            load_hid(i).wait()
        if i == 0:
            load_wkv().start()
        elif i <= n_q:
            load_wq(i - 1).start()
        with jax.named_scope('norm'):
            rows = slice(i * ln_rows, (i + 1) * ln_rows)
            per_slab = s_buf.shape[1] // ln_rows * (s_buf.shape[2] // HEAD_DIM)
            def kept(b):
                slab, b = divmod(b, per_slab)
                r, c = divmod(b, s_buf.shape[2] // HEAD_DIM)
                return s_buf.at[slab, r * ln_rows:(r + 1) * ln_rows, c * HEAD_DIM:(c + 1) * HEAD_DIM]
            total = jnp.zeros((ln_rows, HEAD_DIM), F32)
            for b in range(d_model // HEAD_DIM):
                x = hid[rows, b * HEAD_DIM:(b + 1) * HEAD_DIM].astype(F32)
                kept(b)[...] = x
                total = total + x
            mean = jnp.broadcast_to(jnp.sum(total, axis=-1, keepdims=True) / d_model, total.shape)
            total = jnp.zeros((ln_rows, HEAD_DIM), F32)
            for b in range(d_model // HEAD_DIM):
                centered = kept(b)[...] - mean
                kept(b)[...] = centered
                total = total + centered * centered
            variance = jnp.sum(total, axis=-1, keepdims=True) / d_model
            scale = jnp.broadcast_to(lax.rsqrt(variance + LN_EPS), total.shape)
            for b in range(d_model // HEAD_DIM):
                cols = slice(b * HEAD_DIM, (b + 1) * HEAD_DIM)
                normed[rows, cols] = (kept(b)[...] * scale * gain_f[:, cols] + bias_f[:, cols]).astype(BF16)
    for i in range(3, n_q):
        load_wq(i).start()

    seg = seg_ref[...]
    seg_high = (seg // 256).astype(F32)
    seg_low = (seg % 256).astype(F32)
    row_id = lax.broadcasted_iota(jnp.int32, (SEG_ROWS, tok), 0)
    kvbuf[me_c, tok:, :] = jnp.where(row_id == 0, seg_high, jnp.where(row_id == 1, seg_low, 0.0)).astype(BF16)
    seg_f = seg.astype(F32)
    for b in range(tok // 128):
        column = jnp.broadcast_to(seg_f[:, b * 128:(b + 1) * 128], (128, 128)).T
        for s in range(128 // PIECE):
            part = column[s * PIECE:(s + 1) * PIECE]
            segq[b * (128 // PIECE) + s] = jnp.concatenate([part] * (tok // 128), axis=1)

    with jax.named_scope('wkv_wait'):
        load_wkv().wait()
    kv = (jnp.dot(normed[...], wkv[...], preferred_element_type=F32) + bkv_ref[...].astype(F32).reshape(1, 2 * HEAD_DIM)).astype(BF16)
    kvbuf[me_c, :tok, :] = kv
    k_ref[...] = kv[:, :HEAD_DIM]
    v_ref[...] = kv[:, HEAD_DIM:]
    with jax.named_scope('barrier_wait'):
        pl.semaphore_wait(barrier, len(peers))

    def send_kv(block, target, send_sem):
        return pltpu.make_async_remote_copy(src_ref=kvbuf.at[block], dst_ref=kvbuf.at[block], send_sem=send_sem,
                                            recv_sem=kv_recv.at[block], device_id={'cp': target}, device_id_type=MESH_ID)
    for d in range(n_chip - 1, 0, -1):
        @pl.when(chip + d < n_chip)
        def _(d=d):
            send_kv(me_c, (me_c + 2 * d) % n_cp, kv_send.at[d]).start()
    @pl.when(core == 0)
    def _():
        send_kv(me_c, sibling, kv_send.at[0]).start()

    bo_f[...] = bo_ref[...].astype(F32).reshape(bo_f.shape)
    bq_f[...] = bq_ref[...].astype(F32).reshape(bq_f.shape)
    for i in range(n_q):
        with jax.named_scope('wq_wait'):
            load_wq(i).wait()
        if i == 0:
            for j in range(8):
                load_wo(j).start()
        q = (jnp.dot(normed[...], wq[i], preferred_element_type=F32) + bq_f[:, i * q_cols:(i + 1) * q_cols]).astype(BF16)
        for piece in range(n_piece):
            for h in range(q_cols // HEAD_DIM):
                head = i * q_cols // HEAD_DIM + h
                q_s[piece, head * PIECE:(head + 1) * PIECE, :] = q[piece * PIECE:(piece + 1) * PIECE, h * HEAD_DIM:(h + 1) * HEAD_DIM]

    def score(piece, blocks, own=None, first=False):
        tops = [] if first else [m_s[...]]
        for block in blocks:
            digits = kvbuf[block, tok:, :].astype(F32)
            visible = segq[piece] == digits[0:1] * 256.0 + digits[1:2]
            if block is own:
                q_pos = lax.broadcasted_iota(jnp.int32, (PIECE, tok), 0) + piece * PIECE
                visible = visible & (lax.broadcasted_iota(jnp.int32, (PIECE, tok), 1) <= q_pos)
            s = lax.dot_general(q_s[piece], kvbuf[block, :tok, :HEAD_DIM], (((1,), (1,)), ((), ())), preferred_element_type=F32)
            s = jnp.where(visible[None], s.reshape(n_heads, PIECE, tok), -jnp.inf).reshape(n_heads * PIECE, tok)
            s_buf[block] = s
            tops += [s[:, b:b + HEAD_DIM] for b in range(0, tok, HEAD_DIM)]
        m_s[...] = functools.reduce(jnp.maximum, tops)

    def weigh(block):
        top = m_s[...]
        parts = [jnp.exp2((s_buf[block, :, b:b + HEAD_DIM] - top) * SCORE_EXP2) for b in range(0, tok, HEAD_DIM)]
        out = jnp.dot(jnp.concatenate(parts, axis=1).astype(BF16), kvbuf[block, :tok, HEAD_DIM:], preferred_element_type=F32)
        return sum(parts), out

    def weigh_pair(i):
        l_first, out_first = weigh(2 * i)
        l_second, out_second = weigh(2 * i + 1)
        l_s[...] += l_first + l_second
        acc_s[...] += out_first + out_second

    def attention_out(piece):
        m_s[...] = jnp.broadcast_to(jnp.max(m_s[...], axis=-1, keepdims=True), m_s.shape)
        @pl.when(core == 0)
        def _():
            l_own, out_own = weigh(me_c)
            l_s[...] = l_own
            acc_s[...] = out_own
        @pl.when(core == 1)
        def _():
            l_s[...] = jnp.zeros_like(l_s)
            acc_s[...] = jnp.zeros_like(acc_s)
        each(0, chip + core, weigh_pair)
        attn = (acc_s[...] / jnp.sum(l_s[...], axis=-1, keepdims=True)).astype(BF16)
        for h in range(n_heads):
            o_s[piece, :, h * HEAD_DIM:(h + 1) * HEAD_DIM] = attn[h * PIECE:(h + 1) * PIECE]

    def score_near(piece):
        @pl.when(core == 0)
        def _():
            score(piece, [me_c], own=me_c, first=True)
        @pl.when(core == 1)
        def _():
            score(piece, [me_c, sibling], own=me_c, first=True)

    def forward(i):
        with jax.named_scope('far_wait_ici'):
            passing = send_kv(me_c - 2 * (i + 1), sibling, fwd_send.at[i])
            passing.wait_recv()
            passing.start()

    def score_far(piece, i, fresh):
        same = me_c - 2 * (i + 1)
        other = sibling - 2 * (i + 1)
        if fresh:
            with jax.named_scope('far_wait_sib'):
                send_kv(other, sibling, fwd_send.at[i]).wait_recv()
        score(piece, [same, other])

    @pl.when(core == 1)
    def _():
        send_kv(sibling, sibling, kv_send.at[0]).wait_recv()
    each(0, jnp.minimum(chip, 2), forward)
    with jax.named_scope('score_near'):
        score_near(0)
    each(jnp.minimum(chip, 2), chip, forward)
    with jax.named_scope('score_far'):
        each(0, chip, lambda i: score_far(0, i, True))

    def message(piece, i):
        target = (me_t + 1 + (i % 2) * (n_tp - 2)) % n_tp
        return pltpu.make_async_remote_copy(src_ref=stage.at[piece, i], dst_ref=recv.at[piece, i], send_sem=msg_send.at[piece, i],
                                            recv_sem=msg_recv.at[piece, i], device_id={'tp': target}, device_id_type=MESH_ID)
    def y_part(piece, owner, part):
        return y_v.at[pl.ds(pl.multiple_of(piece * PIECE, PIECE), PIECE), pl.ds(pl.multiple_of(owner * chunk + part * half, 128), half)]
    def gather(piece, way, part):
        ref = y_part(piece, me_t, part)
        return pltpu.make_async_remote_copy(src_ref=ref, dst_ref=ref, send_sem=ag_send.at[piece, way, part],
                                            recv_sem=ag_recv.at[piece, way, part], device_id={'tp': (right, left)[way]}, device_id_type=MESH_ID)
    def pass_on(piece, way):
        ref = y_part(piece, (left, right)[way], way)
        return pltpu.make_async_remote_copy(src_ref=ref, dst_ref=ref, send_sem=fw_send.at[piece, way],
                                            recv_sem=fw_recv.at[piece, way], device_id={'tp': (right, left)[way]}, device_id_type=MESH_ID)

    def project_first(s):
        def one(i):
            @pl.when(s == 0)
            def _():
                wait_wo(i)
            stage[s, i] = jnp.dot(o_s[s], wo[i], preferred_element_type=F32).astype(BF16)
            message(s, i).start()
        with jax.named_scope('project_first'):
            each(0, 4, one)

    def project_rest(piece, fresh):
        def one(i):
            if fresh is not None:
                @pl.when(fresh)
                def _():
                    wait_wo(i)
            stage[piece, i] = jnp.dot(o_s[piece], wo[i], preferred_element_type=F32).astype(BF16)
            @pl.when(i < 6)
            def _():
                with jax.named_scope('E_wait'):
                    message(piece, i - 4).wait_recv()
                stage[piece, i] = (stage[piece, i].astype(F32) + recv[piece, i - 4].astype(F32)).astype(BF16)
                message(piece, i).start()
        with jax.named_scope('project_rest'):
            each(4, 8, one)

    def add_up(piece):
        with jax.named_scope('G_wait'):
            for i in range(2, 6):
                message(piece, i).wait_recv()
        rows = pl.ds(pl.multiple_of(piece * PIECE, PIECE), PIECE)
        for part in range(2):
            cols = pl.ds(pl.multiple_of(me_t * chunk + part * half, 128), half)
            from_left, from_right = ((4, 3), (2, 5))[part]
            proj = stage[piece, 6 + part].astype(F32) + recv[piece, from_left].astype(F32) + recv[piece, from_right].astype(F32)
            y_v[rows, cols] = (hid[rows, cols].astype(F32) + proj + bo_f[:, cols]).astype(BF16)
            for way in range(2):
                gather(piece, way, part).start()

    def hand_on(piece):
        for way in range(2):
            with jax.named_scope('H_wait'):
                gather(piece, way, way).wait_recv()
            pass_on(piece, way).start()

    def step(s):
        with jax.named_scope('rest_score'):
            @pl.when(s > 0)
            def _():
                score_near(s)
                each(0, chip, lambda i: score_far(s, i, False))
        with jax.named_scope('weigh'):
            attention_out(s)
        project_first(s)
        @pl.when(s == 2)
        def _():
            add_up(0)
        @pl.when(s > 0)
        def _():
            project_rest(s - 1, s == 1)
    each(0, n_piece, step)
    project_rest(n_piece - 1, None)
    each(1, n_piece - 1, add_up)
    hand_on(0)
    add_up(n_piece - 1)
    each(1, n_piece, hand_on)
    with jax.named_scope('I_wait'):
        def arrived(piece):
            for way in range(2):
                gather(piece, way, 1 - way).wait_recv()
                pass_on(piece, way).wait_recv()
        each(0, n_piece, arrived)

    def finish(piece):
        for i in range(6):
            message(piece, i).wait_send()
        for way in range(2):
            for part in range(2):
                gather(piece, way, part).wait_send()
            pass_on(piece, way).wait_send()
    with jax.named_scope('finish'):
        each(0, n_piece, finish)
    for d in range(n_chip - 1, 0, -1):
        @pl.when(chip + d < n_chip)
        def _(d=d):
            send_kv(me_c, (me_c + 2 * d) % n_cp, kv_send.at[d]).wait_send()
    @pl.when(core == 0)
    def _():
        send_kv(me_c, sibling, kv_send.at[0]).wait_send()
    each(0, chip, lambda i: send_kv(me_c - 2 * (i + 1), sibling, fwd_send.at[i]).wait_send())


def store_kernel(*refs):
    copies = [pltpu.make_async_copy(refs[i], refs[3 + i], refs[6].at[i]) for i in range(3)]
    for copy in copies:
        copy.start()
    for copy in copies:
        copy.wait()


def solution(mesh):
    n_tp, n_cp = mesh.shape['tp'], mesh.shape['cp']

    def local_block(hidden, seg_ids, w_q, b_q, w_kv, b_kv, w_o, b_o, ln_gain, ln_bias):
        tok, d_model = hidden.shape
        width = w_q.shape[1]
        n_piece = tok // PIECE
        n_heads = width // HEAD_DIM
        rows = n_heads * PIECE
        half = d_model // n_tp // 2
        hbm = pl.BlockSpec(memory_space=pl.ANY)
        vmem = pl.BlockSpec(memory_space=pltpu.VMEM)
        dma = pltpu.SemaphoreType.DMA
        scratch = [
            pltpu.VMEM((tok, d_model), BF16),
            pltpu.VMEM((1, d_model), F32),
            pltpu.VMEM((1, d_model), F32),
            pltpu.VMEM((1, width), F32),
            pltpu.VMEM((1, d_model), F32),
            pltpu.VMEM((d_model, 2 * HEAD_DIM), BF16),
            pltpu.VMEM((width // Q_COLS, d_model, Q_COLS), BF16),
            pltpu.VMEM((2 * n_tp, width, half), BF16),
            pltpu.VMEM((n_cp, tok + SEG_ROWS, 2 * HEAD_DIM), BF16),
            pltpu.VMEM((n_piece, PIECE, tok), F32),
            pltpu.VMEM((n_piece, rows, HEAD_DIM), BF16),
            pltpu.VMEM((n_cp, rows, tok), F32),
            pltpu.VMEM((rows, HEAD_DIM), F32),
            pltpu.VMEM((rows, HEAD_DIM), F32),
            pltpu.VMEM((rows, HEAD_DIM), F32),
            pltpu.VMEM((n_piece, PIECE, width), BF16),
            pltpu.VMEM((n_piece, 8, PIECE, half), BF16),
            pltpu.VMEM((n_piece, 6, PIECE, half), BF16),
            dma((4,)), dma, dma((width // Q_COLS,)), dma((8,)),
            dma((n_cp // 2,)), dma((n_cp // 2,)), dma((n_cp,)), dma((n_piece, 6)), dma((n_piece, 6)),
            dma((n_piece, 2, 2)), dma((n_piece, 2, 2)), dma((n_piece, 2)), dma((n_piece, 2)),
        ]
        row = lambda a: a.reshape(1, a.shape[0])
        outs = pl.pallas_call(
            functools.partial(block_kernel, n_tp, n_cp),
            out_shape=(pltpu.VMEM((tok, d_model), BF16), pltpu.VMEM((tok, HEAD_DIM), BF16), pltpu.VMEM((tok, HEAD_DIM), BF16)),
            in_specs=[hbm, vmem, hbm, vmem, hbm, vmem, hbm, vmem, vmem, vmem],
            out_specs=(vmem, vmem, vmem),
            scratch_shapes=scratch,
            compiler_params=pltpu.CompilerParams(collective_id=0, has_side_effects=True, vmem_limit_bytes=VMEM_LIMIT),
            name='attention_block',
        )(hidden, row(seg_ids), w_q, b_q, w_kv, b_kv, w_o, b_o, ln_gain, ln_bias)
        return pl.pallas_call(
            store_kernel,
            out_shape=tuple(jax.ShapeDtypeStruct(a.shape, a.dtype) for a in outs),
            in_specs=[vmem] * 3, out_specs=(hbm,) * 3,
            scratch_shapes=[dma((3,))],
            compiler_params=pltpu.CompilerParams(vmem_limit_bytes=2 ** 20),
            name='store_outputs',
        )(*[pltpu.with_memory_space_constraint(a, pltpu.VMEM) for a in outs])

    row_spec = P(('dp', 'cp'), None)
    tok_spec = P(('dp', 'cp'))
    return jax.shard_map(local_block, mesh=mesh,
                         in_specs=(row_spec, tok_spec, P(None, 'tp'), P('tp'), P(None, None), P(None), P('tp', None), P(None), P(None), P(None)),
                         out_specs=(row_spec, row_spec, row_spec), check_vma=False)
```

time: 109 us -> 79 us (0.72)
  Pallas kernels: 95.9 us -> 77.5 us
  local copies, waits for them, and re-layouts: 11.7 us -> 0 us
    pallas_call x1 -> x2, Pallas kernels: 95.9 us -> 77.5 us  [the longest x1 75.7 us: local_block(): pl.pallas_call(functools.partial(block_kernel, n_tp, n_cp), out_shape=(pl...]
    reshape x5 -> x0, local copies, waits for them, and re-layouts: 6.5 us -> none  [local_block(): row = lambda a: a.reshape(1, a.shape[0])]
    unnamed x7 -> x0, local copies, waits for them, and re-layouts: 5.18 us -> none
where the time goes in v2:
time: 79 us; the launch traced here: 78.1 us
  Pallas kernels  77.5 us (98%)
    pallas_call x1, Pallas kernels, local_block(): pl.pallas_call(functools.partial(block_kernel, n_tp, n_cp), out_shape=(pl...  75.7 us
    pallas_call x1, Pallas kernels, local_block(): pl.pallas_call(store_kernel, out_shape=tuple((jax.ShapeDtypeStruct(a.shap...  1.71 us

profile of v2, /device:TPU:102, one launch (start us, length us, event | category | flops | bytes accessed | tf_op | source)
XLA Modules:
  0.0 78.1 jit_solution(11014660125716616370)
XLA Ops:
  0.6 75.7 %attention_block.1 = (bf16[256,6144]{1,0:T(8,128)(2,1)S(1)}, bf16[256,128]{1,0:T(8,128)(2,1)S(1)}, bf16[256,128]{1,0:T(8,128)(2,1)S(1)}) custom-call(bf16[256,6144]{1,0:T(8,128)(2,1)} %hid_hbm.1, s32[1,256]{1,0:T(1,128)} %bitcast.1, bf16[6144,1536]{1,0:T(8,128)(2,1)} %wq_hbm.1, bf16[1536]{0:T(1024)(128)(2,1)} %bq_ref.1, bf16[6144,256]{1,0:T(8,128)(2,1)} %wkv_hbm.1, ...), custom_call_target="tpu_custom_call" | custom-call | tf_op jit(solution)/shard_map/attention_block/pallas_call | solution.py:382
  76.4 1.7 %store_outputs.1 = (bf16[256,6144]{1,0:T(8,128)(2,1)}, bf16[256,128]{1,0:T(8,128)(2,1)}, bf16[256,128]{1,0:T(8,128)(2,1)}) custom-call(bf16[256,6144]{1,0:T(8,128)(2,1)S(1)} %get-tuple-element.6.refs_0_, bf16[256,128]{1,0:T(8,128)(2,1)S(1)} %get-tuple-element.7.refs_1_, bf16[256,128]{1,0:T(8,128)(2,1)S(1)} %get-tuple-element.8.refs_2_), custom_call_target="tpu_custom_call" | custom-call | tf_op jit(solution)/shard_map/store_outputs/pallas_call | solution.py:391

commit v3 on v2

--- a/solution.py
+++ b/solution.py
@@ -12,6 +12,8 @@
 SCORE_EXP2 = HEAD_DIM ** -0.5 * 1.4426950408889634
 PIECE = 64
 Q_COLS = 512
+SCORE_HEADS = 6
+WEIGH_HEADS = 6
 VMEM_LIMIT = 60 * 2 ** 20
 SEG_ROWS = 16
 MESH_ID = pl.DeviceIdType.MESH
@@ -26,10 +28,10 @@
     lax.fori_loop(lo, hi, step, 0)
 
 
-def block_kernel(n_tp, n_cp, hid_hbm, seg_ref, wq_hbm, bq_ref, wkv_hbm, bkv_ref, wo_hbm, bo_ref, gain_ref, lnb_ref,
+def block_kernel(n_tp, n_cp, hid_hbm, seg_hbm, wq_hbm, bq_hbm, wkv_hbm, bkv_hbm, wo_hbm, bo_hbm, gain_hbm, lnb_hbm,
                  y_v, k_ref, v_ref,
-                 normed, gain_f, bias_f, bq_f, bo_f, wkv, wq, wo, kvbuf, segq, q_s, s_buf, m_s, l_s, acc_s, o_s, stage, recv,
-                 hid_sem, wkv_sem, wq_sem, wo_sem, kv_send, fwd_send, kv_recv, msg_send, msg_recv,
+                 seg_ref, bq_ref, bkv_ref, bo_ref, gain_ref, lnb_ref, normed, gain_f, bias_f, bq_f, bo_f, wkv, wq, wo, kvbuf, segq, q_s, s_buf, m_s, l_s, acc_s, o_s, stage, recv,
+                 small_sem, hid_sem, wkv_sem, wq_sem, wo_sem, kv_send, fwd_send, kv_recv, msg_send, msg_recv,
                  ag_send, ag_recv, fw_send, fw_recv):
     hid = y_v
     tok, d_model = hid.shape
@@ -51,8 +53,10 @@
 
     ln_rows = tok // 4
     def load_hid(i):
-        rows = pl.ds(i * ln_rows, ln_rows)
-        return pltpu.make_async_copy(hid_hbm.at[rows, :], hid.at[rows, :], hid_sem.at[i])
+        parts = [(i + 3, i * ln_rows, ln_rows)] if i else [(j, j * ln_rows // 4, ln_rows // 4) for j in range(4)]
+        return [pltpu.make_async_copy(hid_hbm.at[pl.ds(at, n), :], hid.at[pl.ds(at, n), :], hid_sem.at[j]) for j, at, n in parts]
+    small = [pltpu.make_async_copy(src, dst, small_sem.at[i]) for i, (src, dst) in enumerate((
+        (gain_hbm, gain_ref), (lnb_hbm, lnb_ref), (seg_hbm, seg_ref), (bkv_hbm, bkv_ref), (bq_hbm, bq_ref), (bo_hbm, bo_ref)))]
     def load_wkv():
         return pltpu.make_async_copy(wkv_hbm, wkv, wkv_sem)
     def load_wq(i):
@@ -65,46 +69,62 @@
     def wait_wo(i):
         pltpu.make_async_copy(wo_hbm.at[:, pl.ds(0, half)], wo.at[i], wo_sem.at[i]).wait()
     for i in range(4):
-        load_hid(i).start()
+        for copy in load_hid(i):
+            copy.start()
+        if i == 0:
+            for copy in small:
+                copy.start()
 
     barrier = pltpu.get_barrier_semaphore()
     peers = [{'tp': left}, {'tp': right}, {'cp': sibling}] + [{'cp': (me_c + 2 * d) % n_cp} for d in range(1, n_chip)]
     for peer in peers:
         pl.semaphore_signal(barrier, inc=1, device_id=peer, device_id_type=MESH_ID)
 
-    gain_f[...] = gain_ref[...].astype(F32).reshape(gain_f.shape)
-    bias_f[...] = lnb_ref[...].astype(F32).reshape(bias_f.shape)
-    for i in range(4):
-        with jax.named_scope('hid_wait'):
-            load_hid(i).wait()
+    def norm_rows(i):
+        rows = slice(i * ln_rows, (i + 1) * ln_rows)
+        per_slab = s_buf.shape[1] // ln_rows * (s_buf.shape[2] // HEAD_DIM)
+        n_col = d_model // HEAD_DIM
+        def kept(b):
+            slab, b = divmod(b + i * n_col, per_slab)
+            r, c = divmod(b, s_buf.shape[2] // HEAD_DIM)
+            return s_buf.at[slab, r * ln_rows:(r + 1) * ln_rows, c * HEAD_DIM:(c + 1) * HEAD_DIM]
+        total = jnp.zeros((ln_rows, HEAD_DIM), F32)
+        for b in range(n_col):
+            x = hid[rows, b * HEAD_DIM:(b + 1) * HEAD_DIM].astype(F32)
+            kept(b)[...] = x
+            total = total + x
+        mean = jnp.broadcast_to(jnp.sum(total, axis=-1, keepdims=True) / d_model, total.shape)
+        total = jnp.zeros((ln_rows, HEAD_DIM), F32)
+        for b in range(n_col):
+            centered = kept(b)[...] - mean
+            kept(b)[...] = centered
+            total = total + centered * centered
+        variance = jnp.sum(total, axis=-1, keepdims=True) / d_model
+        scale = jnp.broadcast_to(lax.rsqrt(variance + LN_EPS), total.shape)
         if i == 0:
-            load_wkv().start()
-        elif i <= n_q:
-            load_wq(i - 1).start()
-        with jax.named_scope('norm'):
-            rows = slice(i * ln_rows, (i + 1) * ln_rows)
-            per_slab = s_buf.shape[1] // ln_rows * (s_buf.shape[2] // HEAD_DIM)
-            def kept(b):
-                slab, b = divmod(b, per_slab)
-                r, c = divmod(b, s_buf.shape[2] // HEAD_DIM)
-                return s_buf.at[slab, r * ln_rows:(r + 1) * ln_rows, c * HEAD_DIM:(c + 1) * HEAD_DIM]
-            total = jnp.zeros((ln_rows, HEAD_DIM), F32)
-            for b in range(d_model // HEAD_DIM):
-                x = hid[rows, b * HEAD_DIM:(b + 1) * HEAD_DIM].astype(F32)
-                kept(b)[...] = x
-                total = total + x
-            mean = jnp.broadcast_to(jnp.sum(total, axis=-1, keepdims=True) / d_model, total.shape)
-            total = jnp.zeros((ln_rows, HEAD_DIM), F32)
-            for b in range(d_model // HEAD_DIM):
-                centered = kept(b)[...] - mean
-                kept(b)[...] = centered
-                total = total + centered * centered
-            variance = jnp.sum(total, axis=-1, keepdims=True) / d_model
-            scale = jnp.broadcast_to(lax.rsqrt(variance + LN_EPS), total.shape)
-            for b in range(d_model // HEAD_DIM):
-                cols = slice(b * HEAD_DIM, (b + 1) * HEAD_DIM)
-                normed[rows, cols] = (kept(b)[...] * scale * gain_f[:, cols] + bias_f[:, cols]).astype(BF16)
-    for i in range(3, n_q):
+            for copy in small:
+                copy.wait()
+            gain_f[...] = gain_ref[...].astype(F32).reshape(gain_f.shape)
+            bias_f[...] = lnb_ref[...].astype(F32).reshape(bias_f.shape)
+        for b in range(n_col):
+            cols = slice(b * HEAD_DIM, (b + 1) * HEAD_DIM)
+            normed[rows, cols] = (kept(b)[...] * scale * gain_f[:, cols] + bias_f[:, cols]).astype(BF16)
+
+    with jax.named_scope('hid_wait'):
+        for copy in load_hid(0):
+            copy.wait()
+    load_wkv().start()
+    load_wq(0).start()
+    with jax.named_scope('norm'):
+        norm_rows(0)
+    with jax.named_scope('hid_wait'):
+        for i in range(1, 4):
+            for copy in load_hid(i):
+                copy.wait()
+    with jax.named_scope('norm'):
+        for i in range(1, 4):
+            norm_rows(i)
+    for i in range(1, n_q):
         load_wq(i).start()
 
     seg = seg_ref[...]
@@ -138,6 +158,12 @@
     @pl.when(core == 0)
     def _():
         send_kv(me_c, sibling, kv_send.at[0]).start()
+
+    def forward(i):
+        with jax.named_scope('far_wait_ici'):
+            passing = send_kv(me_c - 2 * (i + 1), sibling, fwd_send.at[i])
+            passing.wait_recv()
+            passing.start()
 
     bo_f[...] = bo_ref[...].astype(F32).reshape(bo_f.shape)
     bq_f[...] = bq_ref[...].astype(F32).reshape(bq_f.shape)
@@ -154,43 +180,46 @@
                 q_s[piece, head * PIECE:(head + 1) * PIECE, :] = q[piece * PIECE:(piece + 1) * PIECE, h * HEAD_DIM:(h + 1) * HEAD_DIM]
 
     def score(piece, blocks, own=None, first=False):
-        tops = [] if first else [m_s[...]]
+        hides = []
         for block in blocks:
             digits = kvbuf[block, tok:, :].astype(F32)
             visible = segq[piece] == digits[0:1] * 256.0 + digits[1:2]
             if block is own:
                 q_pos = lax.broadcasted_iota(jnp.int32, (PIECE, tok), 0) + piece * PIECE
                 visible = visible & (lax.broadcasted_iota(jnp.int32, (PIECE, tok), 1) <= q_pos)
-            s = lax.dot_general(q_s[piece], kvbuf[block, :tok, :HEAD_DIM], (((1,), (1,)), ((), ())), preferred_element_type=F32)
-            s = jnp.where(visible[None], s.reshape(n_heads, PIECE, tok), -jnp.inf).reshape(n_heads * PIECE, tok)
-            s_buf[block] = s
-            tops += [s[:, b:b + HEAD_DIM] for b in range(0, tok, HEAD_DIM)]
-        m_s[...] = functools.reduce(jnp.maximum, tops)
-
-    def weigh(block):
-        top = m_s[...]
-        parts = [jnp.exp2((s_buf[block, :, b:b + HEAD_DIM] - top) * SCORE_EXP2) for b in range(0, tok, HEAD_DIM)]
-        out = jnp.dot(jnp.concatenate(parts, axis=1).astype(BF16), kvbuf[block, :tok, HEAD_DIM:], preferred_element_type=F32)
-        return sum(parts), out
-
-    def weigh_pair(i):
-        l_first, out_first = weigh(2 * i)
-        l_second, out_second = weigh(2 * i + 1)
-        l_s[...] += l_first + l_second
-        acc_s[...] += out_first + out_second
+            hides.append(visible[None])
+        for r in range(0, n_heads, SCORE_HEADS):
+            rows = slice(r * PIECE, (r + SCORE_HEADS) * PIECE)
+            tops = [] if first else [m_s[rows]]
+            for block, visible in zip(blocks, hides):
+                s = lax.dot_general(q_s[piece, rows], kvbuf[block, :tok, :HEAD_DIM], (((1,), (1,)), ((), ())), preferred_element_type=F32)
+                s = jnp.where(visible, (s * SCORE_EXP2).reshape(SCORE_HEADS, PIECE, tok), -jnp.inf).reshape(SCORE_HEADS * PIECE, tok)
+                s_buf[block, rows] = s
+                tops += [s[:, b:b + HEAD_DIM] for b in range(0, tok, HEAD_DIM)]
+            m_s[rows] = functools.reduce(jnp.maximum, tops)
+
+    def weigh_some(blocks):
+        v_all = jnp.concatenate([kvbuf[block, :tok, HEAD_DIM:] for block in blocks], axis=0)
+        for r in range(0, n_heads, WEIGH_HEADS):
+            rows = slice(r * PIECE, (r + WEIGH_HEADS) * PIECE)
+            top = m_s[rows]
+            parts = [jnp.exp2(s_buf[block, rows, b:b + HEAD_DIM] - top) for block in blocks for b in range(0, tok, HEAD_DIM)]
+            l_s[rows] += sum(parts)
+            acc_s[rows] += jnp.dot(jnp.concatenate(parts, axis=1).astype(BF16), v_all, preferred_element_type=F32)
 
     def attention_out(piece):
         m_s[...] = jnp.broadcast_to(jnp.max(m_s[...], axis=-1, keepdims=True), m_s.shape)
-        @pl.when(core == 0)
-        def _():
-            l_own, out_own = weigh(me_c)
-            l_s[...] = l_own
-            acc_s[...] = out_own
-        @pl.when(core == 1)
-        def _():
-            l_s[...] = jnp.zeros_like(l_s)
-            acc_s[...] = jnp.zeros_like(acc_s)
-        each(0, chip + core, weigh_pair)
+        l_s[...] = jnp.zeros_like(l_s)
+        acc_s[...] = jnp.zeros_like(acc_s)
+        n_block = me_c + 1
+        each(0, n_block // 4, lambda i: weigh_some([4 * i + j for j in range(4)]))
+        @pl.when(n_block % 4 >= 2)
+        def _():
+            at = n_block // 4 * 4
+            weigh_some([at, at + 1])
+        @pl.when(n_block % 2 == 1)
+        def _():
+            weigh_some([me_c])
         attn = (acc_s[...] / jnp.sum(l_s[...], axis=-1, keepdims=True)).astype(BF16)
         for h in range(n_heads):
             o_s[piece, :, h * HEAD_DIM:(h + 1) * HEAD_DIM] = attn[h * PIECE:(h + 1) * PIECE]
@@ -203,19 +232,12 @@
         def _():
             score(piece, [me_c, sibling], own=me_c, first=True)
 
-    def forward(i):
-        with jax.named_scope('far_wait_ici'):
-            passing = send_kv(me_c - 2 * (i + 1), sibling, fwd_send.at[i])
-            passing.wait_recv()
-            passing.start()
-
-    def score_far(piece, i, fresh):
-        same = me_c - 2 * (i + 1)
-        other = sibling - 2 * (i + 1)
-        if fresh:
-            with jax.named_scope('far_wait_sib'):
-                send_kv(other, sibling, fwd_send.at[i]).wait_recv()
-        score(piece, [same, other])
+    def far(i):
+        return me_c - 2 * (i + 1), sibling - 2 * (i + 1)
+
+    def wait_passed(i):
+        with jax.named_scope('far_wait_sib'):
+            send_kv(far(i)[1], sibling, fwd_send.at[i]).wait_recv()
 
     @pl.when(core == 1)
     def _():
@@ -225,7 +247,13 @@
         score_near(0)
     each(jnp.minimum(chip, 2), chip, forward)
     with jax.named_scope('score_far'):
-        each(0, chip, lambda i: score_far(0, i, True))
+        def listed(j):
+            here = j < chip
+            @pl.when(j >= chip)
+            def _():
+                wait_passed(j - chip)
+            return jnp.where(here, me_c - 2 * (j + 1), sibling - 2 * (j - chip + 1))
+        each(0, chip, lambda i: score(0, [listed(2 * i), listed(2 * i + 1)]))
 
     def message(piece, i):
         target = (me_t + 1 + (i % 2) * (n_tp - 2)) % n_tp
@@ -242,31 +270,35 @@
         return pltpu.make_async_remote_copy(src_ref=ref, dst_ref=ref, send_sem=fw_send.at[piece, way],
                                             recv_sem=fw_recv.at[piece, way], device_id={'tp': (right, left)[way]}, device_id_type=MESH_ID)
 
-    def project_first(s):
-        def one(i):
-            @pl.when(s == 0)
+    def project(piece):
+        def one(j):
+            i = j + 2 * (j // 2 % 2) - 2 * (j // 4)
+            @pl.when(piece == 0)
             def _():
                 wait_wo(i)
-            stage[s, i] = jnp.dot(o_s[s], wo[i], preferred_element_type=F32).astype(BF16)
-            message(s, i).start()
-        with jax.named_scope('project_first'):
-            each(0, 4, one)
-
-    def project_rest(piece, fresh):
+            stage[piece, i] = jnp.dot(o_s[piece], wo[i], preferred_element_type=F32).astype(BF16)
+            @pl.when(i < 4)
+            def _():
+                message(piece, i).start()
+        with jax.named_scope('project'):
+            each(0, 6, one)
+
+    def relay(piece):
+        for i in range(2):
+            with jax.named_scope('E_wait'):
+                message(piece, i).wait_recv()
+            stage[piece, 4 + i] = (stage[piece, 4 + i].astype(F32) + recv[piece, i].astype(F32)).astype(BF16)
+            message(piece, 4 + i).start()
+
+    def project_own(piece, fresh=None):
         def one(i):
             if fresh is not None:
                 @pl.when(fresh)
                 def _():
                     wait_wo(i)
             stage[piece, i] = jnp.dot(o_s[piece], wo[i], preferred_element_type=F32).astype(BF16)
-            @pl.when(i < 6)
-            def _():
-                with jax.named_scope('E_wait'):
-                    message(piece, i - 4).wait_recv()
-                stage[piece, i] = (stage[piece, i].astype(F32) + recv[piece, i - 4].astype(F32)).astype(BF16)
-                message(piece, i).start()
-        with jax.named_scope('project_rest'):
-            each(4, 8, one)
+        with jax.named_scope('project_own'):
+            each(6, 8, one)
 
     def add_up(piece):
         with jax.named_scope('G_wait'):
@@ -288,26 +320,36 @@
             pass_on(piece, way).start()
 
     def step(s):
-        with jax.named_scope('rest_score'):
-            @pl.when(s > 0)
-            def _():
+        @pl.when(s > 0)
+        def _():
+            with jax.named_scope('rest_score'):
                 score_near(s)
-                each(0, chip, lambda i: score_far(s, i, False))
+                each(0, chip, lambda i: score(s, far(i)))
+            relay(s - 1)
         with jax.named_scope('weigh'):
             attention_out(s)
-        project_first(s)
-        @pl.when(s == 2)
-        def _():
-            add_up(0)
+        project(s)
         @pl.when(s > 0)
         def _():
-            project_rest(s - 1, s == 1)
+            project_own(s - 1, s == 1)
+        @pl.when((s > 0) & (s < n_piece - 1))
+        def _():
+            add_up(s - 1)
     each(0, n_piece, step)
-    project_rest(n_piece - 1, None)
-    each(1, n_piece - 1, add_up)
+    last = n_piece - 1
     hand_on(0)
-    add_up(n_piece - 1)
-    each(1, n_piece, hand_on)
+    project_own(last)
+    relay(last)
+    add_up(last - 1)
+    add_up(last)
+    with jax.named_scope('send_wait'):
+        for way in range(2):
+            gather(last, way, 0).wait_send()
+    hand_on(1)
+    with jax.named_scope('send_wait'):
+        for way in range(2):
+            gather(last, way, 1).wait_send()
+    each(2, n_piece, hand_on)
     with jax.named_scope('I_wait'):
         def arrived(piece):
             for way in range(2):
@@ -319,8 +361,10 @@
         for i in range(6):
             message(piece, i).wait_send()
         for way in range(2):
-            for part in range(2):
-                gather(piece, way, part).wait_send()
+            @pl.when(piece < last)
+            def _():
+                for part in range(2):
+                    gather(piece, way, part).wait_send()
             pass_on(piece, way).wait_send()
     with jax.named_scope('finish'):
         each(0, n_piece, finish)
@@ -335,7 +379,10 @@
 
 
 def store_kernel(*refs):
-    copies = [pltpu.make_async_copy(refs[i], refs[3 + i], refs[6].at[i]) for i in range(3)]
+    y_v, k_v, v_v, y_out, k_out, v_out, sem = refs
+    rows = y_v.shape[0] // 4
+    parts = [(y_v.at[pl.ds(i * rows, rows), :], y_out.at[pl.ds(i * rows, rows), :]) for i in range(4)]
+    copies = [pltpu.make_async_copy(src, dst, sem.at[i]) for i, (src, dst) in enumerate(parts + [(k_v, k_out), (v_v, v_out)])]
     for copy in copies:
         copy.start()
     for copy in copies:
@@ -356,6 +403,9 @@
         vmem = pl.BlockSpec(memory_space=pltpu.VMEM)
         dma = pltpu.SemaphoreType.DMA
         scratch = [
+            pltpu.VMEM((1, tok), jnp.int32),
+            pltpu.VMEM(b_q.shape, BF16), pltpu.VMEM(b_kv.shape, BF16), pltpu.VMEM(b_o.shape, BF16),
+            pltpu.VMEM(ln_gain.shape, BF16), pltpu.VMEM(ln_bias.shape, BF16),
             pltpu.VMEM((tok, d_model), BF16),
             pltpu.VMEM((1, d_model), F32),
             pltpu.VMEM((1, d_model), F32),
@@ -374,7 +424,7 @@
             pltpu.VMEM((n_piece, PIECE, width), BF16),
             pltpu.VMEM((n_piece, 8, PIECE, half), BF16),
             pltpu.VMEM((n_piece, 6, PIECE, half), BF16),
-            dma((4,)), dma, dma((width // Q_COLS,)), dma((8,)),
+            dma((6,)), dma((7,)), dma, dma((width // Q_COLS,)), dma((8,)),
             dma((n_cp // 2,)), dma((n_cp // 2,)), dma((n_cp,)), dma((n_piece, 6)), dma((n_piece, 6)),
             dma((n_piece, 2, 2)), dma((n_piece, 2, 2)), dma((n_piece, 2)), dma((n_piece, 2)),
         ]
@@ -382,7 +432,7 @@
         outs = pl.pallas_call(
             functools.partial(block_kernel, n_tp, n_cp),
             out_shape=(pltpu.VMEM((tok, d_model), BF16), pltpu.VMEM((tok, HEAD_DIM), BF16), pltpu.VMEM((tok, HEAD_DIM), BF16)),
-            in_specs=[hbm, vmem, hbm, vmem, hbm, vmem, hbm, vmem, vmem, vmem],
+            in_specs=[hbm] * 10,
             out_specs=(vmem, vmem, vmem),
             scratch_shapes=scratch,
             compiler_params=pltpu.CompilerParams(collective_id=0, has_side_effects=True, vmem_limit_bytes=VMEM_LIMIT),
@@ -392,7 +442,7 @@
             store_kernel,
             out_shape=tuple(jax.ShapeDtypeStruct(a.shape, a.dtype) for a in outs),
             in_specs=[vmem] * 3, out_specs=(hbm,) * 3,
-            scratch_shapes=[dma((3,))],
+            scratch_shapes=[dma((6,))],
             compiler_params=pltpu.CompilerParams(vmem_limit_bytes=2 ** 20),
             name='store_outputs',
         )(*[pltpu.with_memory_space_constraint(a, pltpu.VMEM) for a in outs])

time: 79 us -> 75.9 us (0.961); the launches traced: 78.1 us -> 75.8 us
  Pallas kernels: 77.5 us -> 75.2 us
    pallas_call x1, Pallas kernels: 75.7 us -> 73.5 us  [local_block(): pl.pallas_call(functools.partial(block_kernel, n_tp, n_cp), out_shape=(pl...]
where the time goes in v3:
time: 75.9 us; the launch traced here: 75.8 us
  Pallas kernels  75.2 us (99%)
    pallas_call x1, Pallas kernels, local_block(): pl.pallas_call(functools.partial(block_kernel, n_tp, n_cp), out_shape=(pl...  73.5 us
    pallas_call x1, Pallas kernels, local_block(): pl.pallas_call(store_kernel, out_shape=tuple((jax.ShapeDtypeStruct(a.shap...  1.74 us

profile of v3, /device:TPU:102, one launch (start us, length us, event | category | flops | bytes accessed | tf_op | source)
XLA Modules:
  0.0 75.8 jit_solution(17072497772950728633)
XLA Ops:
  0.6 73.5 %attention_block.1 = (bf16[256,6144]{1,0:T(8,128)(2,1)S(1)}, bf16[256,128]{1,0:T(8,128)(2,1)S(1)}, bf16[256,128]{1,0:T(8,128)(2,1)S(1)}) custom-call(bf16[256,6144]{1,0:T(8,128)(2,1)} %hid_hbm.1, s32[1,256]{1,0:T(1,128)} %bitcast.1, bf16[6144,1536]{1,0:T(8,128)(2,1)} %wq_hbm.1, bf16[1536]{0:T(1024)(128)(2,1)} %bq_hbm.1, bf16[6144,256]{1,0:T(8,128)(2,1)} %wkv_hbm.1, ...), custom_call_target="tpu_custom_call" | custom-call | tf_op jit(solution)/shard_map/attention_block/pallas_call | solution.py:432
  74.1 1.7 %store_outputs.1 = (bf16[256,6144]{1,0:T(8,128)(2,1)}, bf16[256,128]{1,0:T(8,128)(2,1)}, bf16[256,128]{1,0:T(8,128)(2,1)}) custom-call(bf16[256,6144]{1,0:T(8,128)(2,1)S(1)} %get-tuple-element.6.refs_0_, bf16[256,128]{1,0:T(8,128)(2,1)S(1)} %get-tuple-element.7.refs_1_, bf16[256,128]{1,0:T(8,128)(2,1)S(1)} %get-tuple-element.8.refs_2_), custom_call_target="tpu_custom_call" | custom-call | tf_op jit(solution)/shard_map/store_outputs/pallas_call | solution.py:441
